TPU v7x, 32 devices: a 4x4x1 block of a 4x4x8 slice. The times are simulated.
32 devices in a mesh: dp: 1 (over z), cp: 4 (over y), tp: 8 (over x, core).
Axes of the slice: x: 4, y: 4, z: 1, core: 2. Of those that a mesh axis runs over, the one named last changes fastest.
The devices are a block of a 4x4x8 slice.
Arguments:
- x: bfloat16 [1, 8192, 5120], P('dp', ('cp', 'tp'))
- g_attn: bfloat16 [5120], replicated
- w_q: bfloat16 [5120, 32, 128], P(None, 'tp')
- w_k: bfloat16 [5120, 8, 128], P(None, 'tp')
- w_v: bfloat16 [5120, 8, 128], P(None, 'tp')
- w_o: bfloat16 [32, 128, 5120], P('tp')
- g_mlp: bfloat16 [5120], replicated
- w_gate: bfloat16 [5120, 14336], P(None, 'tp')
- w_up: bfloat16 [5120, 14336], P(None, 'tp')
- w_down: bfloat16 [14336, 5120], P('tp')
Outputs:
- output: bfloat16 [1, 8192, 5120], P('dp', ('cp', 'tp'))
All inputs are finite; a program needn't handle non-finite values.
Results may differ from a plain program's by a relative error of at most 0.02.
Values are sent between devices in bfloat16 or wider.
A program may use at most 768 MiB of HBM per device.

v0:
```python
import jax
import jax.numpy as jnp
from jax import lax
from jax.sharding import PartitionSpec as P

NORM_EPS = 1e-5
ROPE_THETA = 500000.0
TILE_ROWS = 256


def rms_norm(rows_in, gain_vec):
    rows_f32 = rows_in.astype(jnp.float32)
    mean_sq = jnp.mean(rows_f32 * rows_f32, axis=-1, keepdims=True)
    return (rows_f32 * lax.rsqrt(mean_sq + NORM_EPS) * gain_vec.astype(jnp.float32)).astype(jnp.bfloat16)


def apply_rope(heads_in, positions):
    head_dim = heads_in.shape[-1]
    half_dim = head_dim // 2
    inv_freq = ROPE_THETA ** (-2.0 * jnp.arange(half_dim, dtype=jnp.float32) / head_dim)
    angles = positions.astype(jnp.float32)[:, None] * inv_freq[None, :]
    angles = jnp.concatenate([angles, angles], axis=-1)[:, None, :]
    heads_f32 = heads_in.astype(jnp.float32)
    rotated = jnp.concatenate([-heads_f32[..., half_dim:], heads_f32[..., :half_dim]], axis=-1)
    return (heads_f32 * jnp.cos(angles) + rotated * jnp.sin(angles)).astype(jnp.bfloat16)


def stored_positions(row_ids, piece_len, cp_size):
    owner_cp = row_ids // (2 * piece_len)
    within = row_ids % (2 * piece_len)
    return jnp.where(within < piece_len, owner_cp * piece_len + within,
                     (2 * cp_size - 1 - owner_cp) * piece_len + within - piece_len)


def attend(q_rows, q_pos, keys, values, key_pos):
    q_len, n_kv_heads, group_size, head_dim = q_rows.shape
    n_tiles = max(1, q_len // TILE_ROWS)
    tile_len = q_len // n_tiles
    score_scale = head_dim ** -0.5

    def one_tile(tile_idx):
        row_start = tile_idx * tile_len
        q_tile = lax.dynamic_slice_in_dim(q_rows, row_start, tile_len, axis=0)
        pos_tile = lax.dynamic_slice_in_dim(q_pos, row_start, tile_len, axis=0)
        scores = jnp.einsum('qgrd,kgd->gqrk', q_tile, keys, preferred_element_type=jnp.float32) * score_scale
        visible = pos_tile[:, None, None] >= key_pos[None, None, :]
        scores = jnp.where(visible, scores, -1e30)
        weights = jnp.exp(scores - jnp.max(scores, axis=-1, keepdims=True))
        row_sum = jnp.sum(weights, axis=-1, keepdims=True)
        mixed_vals = jnp.einsum('gqrk,kgd->gqrd', weights.astype(jnp.bfloat16), values, preferred_element_type=jnp.float32) / row_sum
        return jnp.transpose(mixed_vals, (1, 0, 2, 3)).astype(jnp.bfloat16)

    tiles = lax.map(one_tile, jnp.arange(n_tiles))
    return tiles.reshape(q_len, n_kv_heads * group_size, head_dim)


def solution(mesh):
    cp_size = mesh.shape['cp']
    row_spec = P('dp', ('cp', 'tp'), None)
    head_cols = P(None, 'tp', None)

    def local_layer(x, g_attn, w_q, w_k, w_v, w_o, g_mlp, w_gate, w_up, w_down):
        x_rows = x[0]
        n_kv_local = w_k.shape[1]
        head_dim = w_q.shape[2]
        group_size = w_q.shape[1] // n_kv_local
        cp_index = lax.axis_index('cp')
        normed = lax.all_gather(rms_norm(x_rows, g_attn), 'tp', axis=0, tiled=True)
        seq_local = normed.shape[0]
        piece_len = seq_local // 2
        positions = stored_positions(cp_index * seq_local + jnp.arange(seq_local, dtype=jnp.int32), piece_len, cp_size)
        q_all = apply_rope(jnp.einsum('sd,dhk->shk', normed, w_q, preferred_element_type=jnp.float32).astype(jnp.bfloat16), positions)
        k_all = apply_rope(jnp.einsum('sd,dhk->shk', normed, w_k, preferred_element_type=jnp.float32).astype(jnp.bfloat16), positions)
        v_all = jnp.einsum('sd,dhk->shk', normed, w_v, preferred_element_type=jnp.float32).astype(jnp.bfloat16)
        k_seq = lax.all_gather(k_all, 'cp', axis=0, tiled=False)
        v_seq = lax.all_gather(v_all, 'cp', axis=0, tiled=False)
        key_pos = stored_positions(jnp.arange(cp_size * seq_local, dtype=jnp.int32), piece_len, cp_size).reshape(cp_size, seq_local)
        first_keys = k_seq[:, :piece_len].reshape(cp_size * piece_len, n_kv_local, head_dim)
        first_vals = v_seq[:, :piece_len].reshape(cp_size * piece_len, n_kv_local, head_dim)
        first_pos = key_pos[:, :piece_len].reshape(cp_size * piece_len)
        q_grp = q_all.reshape(seq_local, n_kv_local, group_size, head_dim)
        attn_first = attend(q_grp[:piece_len], positions[:piece_len], first_keys, first_vals, first_pos)
        attn_second = attend(q_grp[piece_len:], positions[piece_len:],
                             k_seq.reshape(cp_size * seq_local, n_kv_local, head_dim),
                             v_seq.reshape(cp_size * seq_local, n_kv_local, head_dim),
                             key_pos.reshape(cp_size * seq_local))
        attn_out = jnp.concatenate([attn_first, attn_second], axis=0)
        attn_part = jnp.einsum('shk,hkd->sd', attn_out, w_o, preferred_element_type=jnp.float32).astype(jnp.bfloat16)
        attn_rows = lax.psum_scatter(attn_part, 'tp', scatter_dimension=0, tiled=True)
        resid_rows = (x_rows.astype(jnp.float32) + attn_rows.astype(jnp.float32)).astype(jnp.bfloat16)
        normed_mlp = lax.all_gather(rms_norm(resid_rows, g_mlp), 'tp', axis=0, tiled=True)
        gate_proj = jnp.dot(normed_mlp, w_gate, preferred_element_type=jnp.float32)
        up_proj = jnp.dot(normed_mlp, w_up, preferred_element_type=jnp.float32)
        hidden = (jax.nn.silu(gate_proj) * up_proj).astype(jnp.bfloat16)
        down_part = jnp.dot(hidden, w_down, preferred_element_type=jnp.float32).astype(jnp.bfloat16)
        down_rows = lax.psum_scatter(down_part, 'tp', scatter_dimension=0, tiled=True)
        z_rows = (resid_rows.astype(jnp.float32) + down_rows.astype(jnp.float32)).astype(jnp.bfloat16)
        return z_rows[None]

    return jax.shard_map(local_layer, mesh=mesh,
                         in_specs=(row_spec, P(), head_cols, head_cols, head_cols, P('tp', None, None),
                                   P(), P(None, 'tp'), P(None, 'tp'), P('tp', None)),
                         out_specs=row_spec, check_vma=False)
```

profile of v0, /device:TPU:97, one launch (start us, length us, event | category | flops | bytes accessed | tf_op | source)
XLA Modules:
  0.0 966.6 jit_solution(1831116673326814401)
XLA Ops:
  6.6 2.4 fusion.89
  9.0 0.7 convert_element_type.107
  9.7 4.0 fusion.91
  14.6 104.1 %all-gather.7.cloned.1.call-done = bf16[2048,5120]{1,0:T(8,128)(2,1)} async-done(((bf16[256,5120]{1,0:T(8,128)(2,1)}), bf16[2048,5120]{1,0:T(8,128)(2,1)}) %all-gather.7.cloned.1.call-update) | async-done | bytes 20971536 | tf_op jit(solution)/shard_map/all_gather | solution.py:68
  118.7 10.7 %convolution_convert_fusion.1 = bf16[2048,128]{1,0:T(8,128)(2,1)} fusion(bf16[2048,5120]{1,0:T(8,128)(2,1)} %all-gather.7.cloned.1.call-done, bf16[5120,1,128]{2,0,1:T(8,128)(2,1)S(1)} %copy-done), kind=kOutput, calls=%fused_computation.82 | convolution fusion | flops 2684616704 | bytes 22806528 | tf_op jit(solution)/shard_map/sd,dhk->shk/dot_general | solution.py:74
  129.6 9.3 copy.11
  139.0 11.2 %fusion.96 = f32[2048,128]{0,1:T(8,128)S(1)} fusion(bf16[2048,5120]{1,0:T(8,128)(2,1)} %all-gather.7.cloned.1.call-done, bf16[5120,1,128]{2,0,1:T(8,128)(2,1)S(1)} %copy-done.4), kind=kOutput, calls=%fused_computation.84 | convolution fusion | flops 2684878848 | bytes 23330816 | tf_op jit(solution)/shard_map/sd,dhk->shk/dot_general | solution.py:73
  150.3 5.0 fusion.105
  155.9 15.7 %fusion.117 = f32[2048,512]{0,1:S(1)} fusion(bf16[2048,5120]{1,0:T(8,128)(2,1)} %all-gather.7.cloned.1.call-done, bf16[5120,512]{0,1:T(8,128)(2,1)} %bitcast.146), kind=kOutput, calls=%fused_computation.136 | convolution fusion | flops 10737418240 | bytes 30408704
  172.2 1.3 fusion.94
  173.4 1.5 slice_bitcast_fusion.1
  174.9 2.4 slice.64
  177.3 10.1 %all-gather.11.cloned.1.call-done = bf16[8192,128]{0,1:T(8,128)(2,1)} async-done(((bf16[2048,128]{0,1:T(8,128)(2,1)}), bf16[8192,128]{0,1:T(8,128)(2,1)}) %all-gather.11.cloned.1.call-update) | async-done | bytes 2097168 | tf_op jit(solution)/shard_map/all_gather | solution.py:75
  187.3 4.2 copy.16
  191.6 2.8 reshape.296
  194.3 1.7 slice.63
  196.0 1.0 copy.12
  197.0 1.2 broadcast.259.clone2.1
  198.2 68.8 %while.21 = (s32[]{:T(128)}, bf16[4,256,1,4,128]{4,1,0,3,2:T(8,128)(2,1)}, s32[4]{0:T(128)S(1)}, s32[1024]{0:T(1024)S(1)}, s32[4,1024]{1,0:T(4,128)S(1)}, /*inde...) while((s32[]{:T(128)}, ...), condition=%wide.region_4.5_spmd, body=%wide.region_1.4_spmd.sunk | while | flops 2194929664 | bytes 57220292 | solution.py:53
  199.6 0.6 broadcast_compare_fusion.5
  200.2 4.5 fusion.143
  204.7 4.5 fusion.144
  209.3 6.2 fusion.145
  216.8 0.6 broadcast_compare_fusion.5
  217.4 4.5 fusion.143
  221.9 4.5 fusion.144
  226.5 6.2 fusion.145
  234.6 4.5 fusion.143
  239.1 4.5 fusion.144
  243.7 6.2 fusion.145
  251.8 4.5 fusion.143
  256.3 4.5 fusion.144
  260.8 6.2 fusion.145
  267.2 197.5 %while.22 = (s32[]{:T(128)}, bf16[4,256,1,4,128]{4,1,0,3,2:T(8,128)(2,1)S(1)}, s32[4]{0:T(128)S(1)}, s32[1024]{0:T(1024)}, bf16[1024,1,4,128]{0,3,2,1:T(8,128)(2...) while((s32[]{:T(128)}, ...), condition=%wide.region_8.9_spmd.clone, body=%wide.region_5.8_spmd.clone.sunk | while | flops 4389763072 | bytes 113859776 | solution.py:53
  268.6 0.8 dynamic_slice.45
  269.4 1.2 broadcast_compare_fusion.6
  270.6 15.8 %fusion.149 = (f32[256,4]{0,1:T(4,128)S(1)}, f32[256,4,8192]{2,0,1:T(8,128)}) fusion(pred[256,8192]{1,0:T(8,128)(4,1)S(1)} %broadcast_compare_fusion.6, bf16[8192,1,128]{2,0,1:T(8,128)(2,1)} %get-tuple-element.298, bf16[1024,1,4,128]{0,3,2,1:T(8,128)(2,1)} %get-tuple-element.297, s32[]{:T(128)S(6)} %select_n.207), kind=kOutput, calls=%fused_computation.24.clone.1 | convolution fusion | flops 2172648448 | bytes 38014980 | tf_op jit(solution)/shard_map/while/body/eval_jaxpr/qgrd,kgd->gqrk/dot_general | solution.py:45
  286.4 15.1 %fusion.150 = f32[256,4]{0,1:T(4,128)S(1)} fusion(f32[256,4,8192]{2,0,1:T(8,128)} %get-tuple-element.269, f32[256,4]{0,1:T(4,128)S(1)} %get-tuple-element.270, pred[256,8192]{1,0:T(8,128)(4,1)S(1)} %broadcast_compare_fusion.6), kind=kLoop, calls=%fused_computation.25.clone.1 | loop fusion | flops 33553408 | bytes 35659776 | tf_op jit(solution)/shard_map/while/body/eval_jaxpr/reduce_sum | solution.py:49
  301.5 15.3 %fusion.151 = bf16[4,256,1,4,128]{4,1,0,3,2:T(8,128)(2,1)S(1)} fusion(bf16[4,256,1,4,128]{4,1,0,3,2:T(8,128)(2,1)S(1)} %get-tuple-element.283, s32[]{:T(128)S(6)} %copy.33, bf16[8192,1,128]{2,0,1:T(8,128)(2,1)} %get-tuple-element.299, f32[256,4,8192]{2,0,1:T(8,128)} %get-tuple-element.269, f32[256,4]{0,1:T(4,128)S(1)} %get-tuple-element.270, ...), kind=kOutput, calls=%fused_computation.36.clone.1 | convolution fusion | flops 2181300224 | bytes 38019076 | tf_op jit(solution)/shard_map/while/body/eval_jaxpr/gqrk,kgd->gqrd/dot_general | solution.py:50
  317.9 0.8 dynamic_slice.45
  318.7 1.2 broadcast_compare_fusion.6
  319.9 15.8 %fusion.149 = (f32[256,4]{0,1:T(4,128)S(1)}, f32[256,4,8192]{2,0,1:T(8,128)}) fusion(pred[256,8192]{1,0:T(8,128)(4,1)S(1)} %broadcast_compare_fusion.6, bf16[8192,1,128]{2,0,1:T(8,128)(2,1)} %get-tuple-element.298, bf16[1024,1,4,128]{0,3,2,1:T(8,128)(2,1)} %get-tuple-element.297, s32[]{:T(128)S(6)} %select_n.207), kind=kOutput, calls=%fused_computation.24.clone.1 | convolution fusion | flops 2172648448 | bytes 38014980 | tf_op jit(solution)/shard_map/while/body/eval_jaxpr/qgrd,kgd->gqrk/dot_general | solution.py:45
  335.7 15.1 %fusion.150 = f32[256,4]{0,1:T(4,128)S(1)} fusion(f32[256,4,8192]{2,0,1:T(8,128)} %get-tuple-element.269, f32[256,4]{0,1:T(4,128)S(1)} %get-tuple-element.270, pred[256,8192]{1,0:T(8,128)(4,1)S(1)} %broadcast_compare_fusion.6), kind=kLoop, calls=%fused_computation.25.clone.1 | loop fusion | flops 33553408 | bytes 35659776 | tf_op jit(solution)/shard_map/while/body/eval_jaxpr/reduce_sum | solution.py:49
  350.8 15.3 %fusion.151 = bf16[4,256,1,4,128]{4,1,0,3,2:T(8,128)(2,1)S(1)} fusion(bf16[4,256,1,4,128]{4,1,0,3,2:T(8,128)(2,1)S(1)} %get-tuple-element.283, s32[]{:T(128)S(6)} %copy.33, bf16[8192,1,128]{2,0,1:T(8,128)(2,1)} %get-tuple-element.299, f32[256,4,8192]{2,0,1:T(8,128)} %get-tuple-element.269, f32[256,4]{0,1:T(4,128)S(1)} %get-tuple-element.270, ...), kind=kOutput, calls=%fused_computation.36.clone.1 | convolution fusion | flops 2181300224 | bytes 38019076 | tf_op jit(solution)/shard_map/while/body/eval_jaxpr/gqrk,kgd->gqrd/dot_general | solution.py:50
  367.2 0.8 dynamic_slice.45
  368.0 1.2 broadcast_compare_fusion.6
  369.2 15.8 %fusion.149 = (f32[256,4]{0,1:T(4,128)S(1)}, f32[256,4,8192]{2,0,1:T(8,128)}) fusion(pred[256,8192]{1,0:T(8,128)(4,1)S(1)} %broadcast_compare_fusion.6, bf16[8192,1,128]{2,0,1:T(8,128)(2,1)} %get-tuple-element.298, bf16[1024,1,4,128]{0,3,2,1:T(8,128)(2,1)} %get-tuple-element.297, s32[]{:T(128)S(6)} %select_n.207), kind=kOutput, calls=%fused_computation.24.clone.1 | convolution fusion | flops 2172648448 | bytes 38014980 | tf_op jit(solution)/shard_map/while/body/eval_jaxpr/qgrd,kgd->gqrk/dot_general | solution.py:45
  385.0 15.1 %fusion.150 = f32[256,4]{0,1:T(4,128)S(1)} fusion(f32[256,4,8192]{2,0,1:T(8,128)} %get-tuple-element.269, f32[256,4]{0,1:T(4,128)S(1)} %get-tuple-element.270, pred[256,8192]{1,0:T(8,128)(4,1)S(1)} %broadcast_compare_fusion.6), kind=kLoop, calls=%fused_computation.25.clone.1 | loop fusion | flops 33553408 | bytes 35659776 | tf_op jit(solution)/shard_map/while/body/eval_jaxpr/reduce_sum | solution.py:49
  400.1 15.3 %fusion.151 = bf16[4,256,1,4,128]{4,1,0,3,2:T(8,128)(2,1)S(1)} fusion(bf16[4,256,1,4,128]{4,1,0,3,2:T(8,128)(2,1)S(1)} %get-tuple-element.283, s32[]{:T(128)S(6)} %copy.33, bf16[8192,1,128]{2,0,1:T(8,128)(2,1)} %get-tuple-element.299, f32[256,4,8192]{2,0,1:T(8,128)} %get-tuple-element.269, f32[256,4]{0,1:T(4,128)S(1)} %get-tuple-element.270, ...), kind=kOutput, calls=%fused_computation.36.clone.1 | convolution fusion | flops 2181300224 | bytes 38019076 | tf_op jit(solution)/shard_map/while/body/eval_jaxpr/gqrk,kgd->gqrd/dot_general | solution.py:50
  416.6 0.8 dynamic_slice.45
  417.3 1.2 broadcast_compare_fusion.6
  418.6 15.8 %fusion.149 = (f32[256,4]{0,1:T(4,128)S(1)}, f32[256,4,8192]{2,0,1:T(8,128)}) fusion(pred[256,8192]{1,0:T(8,128)(4,1)S(1)} %broadcast_compare_fusion.6, bf16[8192,1,128]{2,0,1:T(8,128)(2,1)} %get-tuple-element.298, bf16[1024,1,4,128]{0,3,2,1:T(8,128)(2,1)} %get-tuple-element.297, s32[]{:T(128)S(6)} %select_n.207), kind=kOutput, calls=%fused_computation.24.clone.1 | convolution fusion | flops 2172648448 | bytes 38014980 | tf_op jit(solution)/shard_map/while/body/eval_jaxpr/qgrd,kgd->gqrk/dot_general | solution.py:45
  434.4 15.1 %fusion.150 = f32[256,4]{0,1:T(4,128)S(1)} fusion(f32[256,4,8192]{2,0,1:T(8,128)} %get-tuple-element.269, f32[256,4]{0,1:T(4,128)S(1)} %get-tuple-element.270, pred[256,8192]{1,0:T(8,128)(4,1)S(1)} %broadcast_compare_fusion.6), kind=kLoop, calls=%fused_computation.25.clone.1 | loop fusion | flops 33553408 | bytes 35659776 | tf_op jit(solution)/shard_map/while/body/eval_jaxpr/reduce_sum | solution.py:49
  449.5 15.3 %fusion.151 = bf16[4,256,1,4,128]{4,1,0,3,2:T(8,128)(2,1)S(1)} fusion(bf16[4,256,1,4,128]{4,1,0,3,2:T(8,128)(2,1)S(1)} %get-tuple-element.283, s32[]{:T(128)S(6)} %copy.33, bf16[8192,1,128]{2,0,1:T(8,128)(2,1)} %get-tuple-element.299, f32[256,4,8192]{2,0,1:T(8,128)} %get-tuple-element.269, f32[256,4]{0,1:T(4,128)S(1)} %get-tuple-element.270, ...), kind=kOutput, calls=%fused_computation.36.clone.1 | convolution fusion | flops 2181300224 | bytes 38019076 | tf_op jit(solution)/shard_map/while/body/eval_jaxpr/gqrk,kgd->gqrd/dot_general | solution.py:50
  464.7 18.2 %bitcast_convert_fusion = bf16[2048,5120]{1,0:T(8,128)(2,1)} fusion(bf16[4,128,5120]{2,1,0:T(8,128)(2,1)} %param.19, bf16[1024,4,128]{2,0,1:T(8,128)(2,1)S(1)} %bitcast.150, bf16[1024,4,128]{2,0,1:T(8,128)(2,1)S(1)} %bitcast.151), kind=kOutput, calls=%fused_computation.61 | convolution fusion | flops 10752098304 | bytes 28311552 | tf_op jit(solution)/shard_map/shk,hkd->sd/dot_general | solution.py:88
  483.7 108.3 %reduce-scatter.3.cloned.1.call-done = bf16[256,5120]{1,0:T(8,128)(2,1)} async-done(((bf16[2048,5120]{1,0:T(8,128)(2,1)}), bf16[256,5120]{1,0:T(8,128)(2,1)}) %reduce-scatter.3.cloned.1.call-update) | async-done | bytes 2621456 | tf_op jit(solution)/shard_map/reduce_scatter | solution.py:89
  592.0 3.6 fusion.85
  595.6 4.4 fusion.87
  600.2 101.0 %all-gather.9.cloned.1.call-done = bf16[2048,5120]{1,0:T(8,128)(2,1)} async-done(((bf16[256,5120]{1,0:T(8,128)(2,1)}), bf16[2048,5120]{1,0:T(8,128)(2,1)}) %all-gather.9.cloned.1.call-update) | async-done | bytes 20971536 | tf_op jit(solution)/shard_map/all_gather | solution.py:91
  701.2 48.1 %fusion.118 = f32[2048,1792]{1,0:T(8,128)} fusion(bf16[2048,5120]{1,0:T(8,128)(2,1)} %all-gather.9.cloned.1.call-done, bf16[5120,1792]{1,0:T(8,128)(2,1)} %param.21), kind=kOutput, calls=%fused_computation.137 | convolution fusion | flops 37580963840 | bytes 54001664 | tf_op jit(solution)/shard_map/dot_general | solution.py:92
  749.3 49.4 %multiply_convert_fusion = bf16[2048,1792]{1,0:T(8,128)(2,1)} fusion(f32[2048,1792]{1,0:T(8,128)} %fusion.118, bf16[2048,5120]{1,0:T(8,128)(2,1)} %all-gather.9.cloned.1.call-done, bf16[5120,1792]{1,0:T(8,128)(2,1)} %param.22), kind=kOutput, calls=%fused_computation.63 | convolution fusion | flops 37602983936 | bytes 61341696 | tf_op jit(solution)/shard_map/dot_general | solution.py:93
  798.7 45.6 %convolution_convert_fusion = bf16[2048,5120]{1,0:T(8,128)(2,1)} fusion(bf16[2048,1792]{1,0:T(8,128)(2,1)} %multiply_convert_fusion, bf16[1792,5120]{1,0:T(8,128)(2,1)} %param.23), kind=kOutput, calls=%fused_computation.62 | convolution fusion | flops 37591449600 | bytes 46661632 | tf_op jit(solution)/shard_map/dot_general | solution.py:95
  844.3 109.1 %reduce-scatter.5.cloned.1.call-done = bf16[256,5120]{1,0:T(8,128)(2,1)} async-done(((bf16[2048,5120]{1,0:T(8,128)(2,1)}), bf16[256,5120]{1,0:T(8,128)(2,1)}) %reduce-scatter.5.cloned.1.call-update) | async-done | bytes 2621456 | tf_op jit(solution)/shard_map/reduce_scatter | solution.py:96
  953.4 6.1 fusion.95
  (69 shorter events, 9.9 us)
Async XLA Ops:
  6.5 112.1 %copy-start = (bf16[5120,1,128]{2,0,1:T(8,128)(2,1)S(1)}, bf16[5120,1,128]{2,0,1:T(8,128)(2,1)}, u32[]{:S(2)}) copy-start(bf16[5120,1,128]{2,0,1:T(8,128)(2,1)} %param.18) | copy-start | bytes 3932164
  6.6 112.1 %all-gather.7.cloned.1.call-start = ((), (), s32[]{:S(2)}) async-start(), calls=%async_computation.2 | async-start | bytes 23592960 | tf_op jit(solution)/shard_map/all_gather | solution.py:68
  13.8 161.1 %all-gather.13.cloned.1.call-start = ((), (), s32[]{:S(2)}) async-start(), calls=%async_computation.7 | async-start | bytes 2621440 | tf_op jit(solution)/shard_map/all_gather | solution.py:76
  129.5 57.9 %all-gather.11.cloned.1.call-start = ((), (), s32[]{:S(2)}) async-start(), calls=%async_computation.6 | async-start | bytes 2621440 | tf_op jit(solution)/shard_map/all_gather | solution.py:75
  129.5 9.5 copy-start.4
  155.3 436.7 %reduce-scatter.3.cloned.1.call-start = ((), (), s32[]{:S(2)}) async-start(), calls=%async_computation.3 | async-start | bytes 23592960 | tf_op jit(solution)/shard_map/reduce_scatter | solution.py:89
  187.3 4.2 copy-start.3
  194.3 3.9 copy-start.5
  267.2 197.5 %copy-start.6 = (bf16[4,256,1,4,128]{4,1,0,3,2:T(8,128)(2,1)S(1)}, bf16[4,256,1,4,128]{4,1,0,3,2:T(8,128)(2,1)}, u32[]{:S(2)}) copy-start(bf16[4,256,1,4,128]{4,1,0,3,2:T(8,128)(2,1)} %get-tuple-element.89) | copy-start | bytes 3145732
  483.0 0.7 copy-start.7
  483.0 218.2 %all-gather.9.cloned.1.call-start = ((), (), s32[]{:S(2)}) async-start(), calls=%async_computation.4 | async-start | bytes 23592960 | tf_op jit(solution)/shard_map/all_gather | solution.py:91
  592.0 3.6 copy-start.2
  600.1 353.3 %reduce-scatter.5.cloned.1.call-start = ((), (), s32[]{:S(2)}) async-start(), calls=%async_computation.5 | async-start | bytes 23592960 | tf_op jit(solution)/shard_map/reduce_scatter | solution.py:96
  844.3 115.2 %copy-start.1 = (bf16[5120,1,128]{2,0,1:T(8,128)(2,1)S(1)}, bf16[5120,1,128]{2,0,1:T(8,128)(2,1)}, u32[]{:S(2)}) copy-start(bf16[5120,1,128]{2,0,1:T(8,128)(2,1)} %param.18) | copy-start | bytes 3932164
Sparse Core Ops, SparseCore 0:
  13.9 104.7 all-gather.6
  129.6 28.1 all-gather.12
  159.3 27.9 all-gather.10
  483.1 108.7 reduce-scatter.2
  600.2 100.9 all-gather.8
  844.5 108.9 reduce-scatter.4
where the time goes:
time: 974 us; the launch traced here: 967 us
  waiting for transfers between devices  433 us (44%)
  matrix products  366 us (38%)
  other arithmetic  114 us (12%)
  local copies, waits for them, and re-layouts  33.5 us (3%)
  between operations  13.9 us (1%)
    reduce_scatter x1, waiting for transfers between devices, local_layer(): lax.psum_scatter(down_part, 'tp', scatter_dimension=0, tiled=True)  109 us
    reduce_scatter x1, waiting for transfers between devices, local_layer(): lax.psum_scatter(attn_part, 'tp', scatter_dimension=0, tiled=True)  108 us
    all_gather x1, waiting for transfers between devices, local_layer(): normed = lax.all_gather(rms_norm(x_rows, g_attn), 'tp', axis=0, tiled=True)  104 us
    all_gather x1, waiting for transfers between devices, local_layer(): lax.all_gather(rms_norm(resid_rows, g_mlp), 'tp', axis=0, tiled=True)  101 us
    dot_general x8, matrix products, one_tile(): jnp.einsum('gqrk,kgd->gqrd', weights.astype(jnp.bfloat16), values, prefer...  85.7 us
    dot_general x8, matrix products, one_tile(): jnp.einsum('qgrd,kgd->gqrk', q_tile, keys, preferred_element_type=jnp.flo...  81.3 us
    reduce_sum x8, other arithmetic, one_tile(): row_sum = jnp.sum(weights, axis=-1, keepdims=True)  78.4 us
    dot_general x1, matrix products, local_layer(): up_proj = jnp.dot(normed_mlp, w_up, preferred_element_type=jnp.float32)  49.4 us
  transfers between devices with their start and end apart: 6, of which 5 were waited for; matrix products, arithmetic and copies ran while one was open for 5% of the time, Pallas kernels for 0%

commit v1 on v0

v1 whole, which is shorter than its diff:
```python
import functools

import jax
import jax.numpy as jnp
from jax import lax
from jax.experimental import pallas as pl
from jax.experimental.pallas import tpu as pltpu
from jax.sharding import PartitionSpec as P

NORM_EPS = 1e-5
ROPE_THETA = 500000.0
MESH = pl.DeviceIdType.MESH
VMEM_LIMIT = 67_000_000
LOG2E = 1.4426950408889634
VM = pl.BlockSpec(memory_space=pltpu.VMEM)
HBM = pl.BlockSpec(memory_space=pl.ANY)


def params(ident):
    return pltpu.CompilerParams(collective_id=ident, has_side_effects=True, vmem_limit_bytes=VMEM_LIMIT)


def remote(src, dst, send_sem, recv_sem, **where):
    return pltpu.make_async_remote_copy(
        src_ref=src, dst_ref=dst, send_sem=send_sem, recv_sem=recv_sem,
        device_id=where, device_id_type=MESH)


def ring(n_tp):
    n_chips = n_tp // 2
    me = lax.axis_index('tp')
    chip, core = me // 2, me % 2
    other = chip * 2 + (1 - core)
    right = ((chip + 1) % n_chips) * 2 + core
    left = ((chip + n_chips - 1) % n_chips) * 2 + core
    return me, chip, core, other, right, left


def greet(barrier, partners):
    for where in partners:
        pl.semaphore_signal(barrier, inc=1, device_id=where, device_id_type=MESH)
    pl.semaphore_wait(barrier, len(partners))


def unit_place(o):
    far = (7 - o) // 6
    near = o // 6
    offset = 2 * far + (1 - far - near) * (1 - 2 * (o % 2))
    half = (o % 2 + ((o // 2) % 2) * (1 - o // 4)) % 2
    return offset, half


def pair_of(b):
    mid = ((b + 1) // 2) % 2
    return mid * b + (1 - mid) * (3 - b)


class Chips:
    def __init__(self, n_tp):
        self.n_chips = n_tp // 2
        self.me, self.chip, self.core, self.other, self.right, self.left = ring(n_tp)

    def place(self, o, flip):
        offset, half = unit_place(o)
        return ((self.chip + offset + self.n_chips) % self.n_chips) * 2 + (self.core + flip) % 2, half


class Gather(Chips):
    def __init__(self, n_tp, src, gath, send_sem, recv_sem):
        super().__init__(n_tp)
        self.src, self.gath, self.send_sem, self.recv_sem = src, gath, send_sem, recv_sem

    @staticmethod
    def sems():
        return [pltpu.SemaphoreType.DMA((2, 4, 4)), pltpu.SemaphoreType.DMA((4, 4))]

    def part(self, b, e):
        return self.gath.at[b, pl.ds(e * 128, 128)]

    def copy(self, src, b, e, dst, lane=1):
        return remote(src, self.part(b, e), self.send_sem.at[lane, b, e], self.recv_sem.at[b, e], tp=dst)

    def start(self, half):
        self.copy(self.src(half), 1, 1 - half, (self.right, self.left)[half]).start()
        self.copy(self.src(half), 0, 2 + half, self.other, 0).start()
        if half:
            self.copy(self.src(1), 2, 1, self.right).start()
            self.copy(self.src(0), 2, 0, self.left).start()

    def take(self, b, flip):
        for i in range(2):
            e = 2 * flip + i
            here = self.part(b, e)
            if flip or b:
                self.copy(here, b, e, self.other).wait_recv()
            if b and not flip:
                if b == 1:
                    self.copy(here, 3, 1 - i, (self.left, self.right)[i]).start()
                self.copy(here, b, 2 + i, self.other, 0).start()

    def finish(self):
        for i in range(2):
            for b in range(4):
                self.copy(self.src(0), b, 2 + i, self.other, 0).wait_send()
                if b:
                    self.copy(self.src(0), b, i, self.other).wait_send()


def chunk(j, size):
    return pl.ds(j * size if isinstance(j, int) else pl.multiple_of(j * size, size), size)


def ag_qkv_kernel(n_tp, n_cp, n_heads, x_ref, g_ref, wq_hbm, wk_hbm, wv_hbm, cos_ref, sin_ref, q_hbm, kv_hbm,
                  gath, wraw, wcat, q_ref, kv_own, ag_send, ag_recv, kv_send, kv_recv, out_sem, local):
    ag = Gather(n_tp, lambda half: gath.at[0, pl.ds(half * 128, 128)], gath, ag_send, ag_recv)
    cp = lax.axis_index('cp')
    up, down = (cp + 1) % n_cp, (cp + n_cp - 1) % n_cp
    hd = 128
    qw = n_heads * hd
    n_pieces = kv_own.shape[0]
    n_steps = n_pieces // 2
    width = gath.shape[2]

    loads = [
        pltpu.make_async_copy(wq_hbm, wraw, local.at[0]),
        pltpu.make_async_copy(wk_hbm, wcat.at[:, pl.ds(qw, hd)], local.at[1]),
        pltpu.make_async_copy(wv_hbm, wcat.at[:, pl.ds(qw + hd, hd)], local.at[2]),
    ]
    for c in loads:
        c.start()

    def norm(half):
        @pl.loop(0, 8)
        def _(r):
            x = x_ref[chunk(half * 8 + r, 16), :].astype(jnp.float32)
            mean_sq = jnp.sum(x * x, axis=-1, keepdims=True) / width
            gath[0, chunk(half * 8 + r, 16), :] = (x * lax.rsqrt(mean_sq + NORM_EPS) * g_ref[0:1, :]).astype(jnp.bfloat16)

    with jax.named_scope('norm'):
        norm(0)
    with jax.named_scope('greet'):
      greet(pltpu.get_barrier_semaphore(), [{'tp': ag.other}, {'tp': ag.right}, {'tp': ag.left}, {'cp': up}, {'cp': down}])
    ag.start(0)
    norm(1)
    ag.start(1)

    def place(n):
        return ag.place(2 * pair_of(n // 4) + n % 2, (n // 2) % 2)

    def kv_piece(where, n):
        slot, half = place(n)
        return kv_hbm.at[where, slot, half]

    def kv_copy(src, where, n, kind, lane, dst):
        return remote(src, kv_piece(where, n), kv_send.at[lane, n], kv_recv.at[kind, n], cp=dst)

    def kv_forward(n):
        kv_copy(kv_own.at[n], down, n, 0, 0, up).wait_recv()
        kv_copy(kv_own.at[n], up, n, 1, 0, up).wait_recv()
        odd = n % 2
        source = down * (1 - odd) + up * odd
        kv_copy(kv_piece(source, n), source, n, 2, 2, up * (1 - odd) + down * odd).start()

    def outs(n):
        slot, half = place(n)
        return (pltpu.make_async_copy(kv_own.at[n], kv_piece(cp, n), out_sem.at[0, n]),
                pltpu.make_async_copy(q_ref.at[n], q_hbm.at[slot, half], out_sem.at[1, n]))

    with jax.named_scope('wload'):
      for c in loads:
        c.wait()

    with jax.named_scope('wcat'):
        @pl.loop(0, wraw.shape[0] // 128)
        def _(i):
            block = wraw[chunk(i, 128)]
            for h in range(n_heads):
                wcat[chunk(i, 128), h * hd:(h + 1) * hd] = block[:, h, :]

    fine = pl.ds(cos_ref.shape[0] - 128, 128)

    @pl.loop(0, n_steps)
    def _(s):
        for k in range(n_steps):
            @pl.when(s == k)
            def _():
                with jax.named_scope(f'take{k}'):
                    ag.take(k // 2, k % 2)
        acc = jnp.dot(gath[s // 2, chunk(s % 2, 256), :], wcat[...], preferred_element_type=jnp.float32)
        for i in range(2):
            n = 2 * s + i
            slot, half = place(n)
            part = acc[i * 128:(i + 1) * 128, :]
            coarse = pl.ds(slot * 2 + half, 1)
            cos0, sin0 = cos_ref[coarse, :], sin_ref[coarse, :]
            cos = cos0 * cos_ref[fine, :] - sin0 * sin_ref[fine, :]
            sin = sin0 * cos_ref[fine, :] + cos0 * sin_ref[fine, :]

            def rope(t):
                t = t.astype(jnp.bfloat16).astype(jnp.float32)
                return (t * cos + pltpu.roll(t, hd // 2, 1) * sin).astype(jnp.bfloat16)

            kv_own[n, 0] = rope(part[:, qw:qw + hd])
            kv_own[n, 1] = part[:, qw + hd:].T.astype(jnp.bfloat16)
            for h in range(n_heads):
                q_ref[n, h] = rope(part[:, h * hd:(h + 1) * hd]).astype(jnp.float32).T.astype(jnp.bfloat16)
        for i in range(2):
            n = 2 * s + i
            kv_copy(kv_own.at[n], cp, n, 0, 0, up).start()
            kv_copy(kv_own.at[n], cp, n, 1, 1, down).start()
            for c in outs(n):
                c.start()

        @pl.when(s >= 2)
        def _():
            kv_forward(2 * s - 4)
            kv_forward(2 * s - 3)

    with jax.named_scope('kvtail'):
        @pl.loop(n_pieces - 4, n_pieces)
        def _(n):
            kv_forward(n)

        @pl.loop(0, n_pieces)
        def _(n):
            kv_copy(kv_own.at[n], (cp + 2) % n_cp, n, 2, 0, up).wait_recv()
            for c in outs(n):
                c.wait()
            for lane in range(3):
                kv_copy(kv_own.at[n], cp, n, 0, lane, up).wait_send()
    ag.finish()


def ag_qkv(x_rows, gains, w_q, w_k, w_v, n_tp, n_cp):
    rows, width = x_rows.shape
    n_heads, hd = w_q.shape[1:]
    bf = jnp.bfloat16
    piece = rows * n_tp // 2
    n = jnp.arange(2 * n_tp, dtype=jnp.int32)
    late = n // n_tp
    cp = lax.axis_index('cp')
    firsts = (cp * (1 - late) + (2 * n_cp - 1 - cp) * late) * piece + (n % n_tp) * 128
    points = jnp.concatenate([firsts, jnp.arange(128, dtype=jnp.int32)]).astype(jnp.float32)
    lane = jnp.arange(hd, dtype=jnp.int32)
    freq = ROPE_THETA ** (-2.0 * (lane % (hd // 2)).astype(jnp.float32) / hd)
    angles = points[:, None] * freq[None, :]
    sign = jnp.where(lane < hd // 2, -1.0, 1.0)
    return pl.pallas_call(
        functools.partial(ag_qkv_kernel, n_tp, n_cp, n_heads),
        out_shape=(jax.ShapeDtypeStruct((n_tp, 2, n_heads, hd, 128), bf),
                   jax.ShapeDtypeStruct((n_cp, n_tp, 2, 2, 128, hd), bf)),
        in_specs=[VM, VM, HBM, HBM, HBM, VM, VM],
        out_specs=(HBM, HBM),
        scratch_shapes=[
            pltpu.VMEM((4, 2 * rows, width), bf),
            pltpu.VMEM(w_q.shape, bf),
            pltpu.VMEM((width, (n_heads + 2) * hd), bf),
            pltpu.VMEM((16, n_heads, hd, 128), bf),
            pltpu.VMEM((16, 2, 128, hd), bf),
            *Gather.sems(),
            pltpu.SemaphoreType.DMA((3, 16)),
            pltpu.SemaphoreType.DMA((3, 16)),
            pltpu.SemaphoreType.DMA((2, 16)),
            pltpu.SemaphoreType.DMA((3,)),
        ],
        compiler_params=params(0),
        name='ag_qkv',
    )(x_rows, gains, w_q, w_k, w_v, jnp.cos(angles), jnp.sin(angles) * sign)


KEY_BLOCK = 512
EXP_ROWS = 64


def attend(q_tile, kv_ref, n_full, shift, n_cp, n_tp, sa_ref, sb_ref, p_ref, acc_ref, m_ref, l_ref):
    hd, nq = q_tile.shape
    c = LOG2E * hd ** -0.5
    per_piece = n_tp * 256 // 2 // KEY_BLOCK

    def place(n):
        piece = n // per_piece
        late = piece // n_cp
        return piece * (1 - late) + (2 * n_cp - 1 - piece) * late, (n % per_piece) * (KEY_BLOCK // 256) + late * (n_tp // 2)

    def scores(n, dst, masked=False):
        j, t = place(n)
        keys = kv_ref[j, pl.ds(t, KEY_BLOCK // 256), :, 0].reshape(KEY_BLOCK, hd)
        s = jnp.dot(keys, q_tile, preferred_element_type=jnp.float32)
        if masked:
            key = lax.broadcasted_iota(jnp.int32, s.shape, 0)
            row = lax.broadcasted_iota(jnp.int32, s.shape, 1) % 128
            s = jnp.where(key <= row + shift, s, -1e30)
        dst[...] = s

    def process(n, s_ref):
        j, t = place(n)
        m8 = jnp.max(s_ref[...].reshape(KEY_BLOCK // 8, 8, nq), axis=0)
        m = m_ref[...]
        m_new = jnp.maximum(m, jnp.max(m8, axis=0, keepdims=True))
        m_ref[...] = m_new
        alpha = jnp.exp2((m - m_new) * c)
        mc = m_new * c
        l8 = l_ref[...] * alpha
        for r in range(0, KEY_BLOCK, EXP_ROWS):
            p = jnp.exp2(s_ref[r:r + EXP_ROWS, :] * c - mc)
            l8 = l8 + jnp.sum(p.reshape(EXP_ROWS // 8, 8, nq), axis=0)
            p_ref[r:r + EXP_ROWS, :] = p.astype(jnp.bfloat16)
        l_ref[...] = l8
        v_t = jnp.concatenate([kv_ref[j, t + i // 2, i % 2, 1] for i in range(KEY_BLOCK // 128)], axis=1)
        acc_ref[...] = acc_ref[...] * alpha + jnp.dot(v_t, p_ref[...], preferred_element_type=jnp.float32)

    acc_ref[...] = jnp.zeros_like(acc_ref)
    m_ref[...] = jnp.full(m_ref.shape, -1e30, jnp.float32)
    l_ref[...] = jnp.zeros_like(l_ref)
    scores(n_full, sa_ref, True)

    @pl.loop(0, n_full // 2)
    def _(k):
        later = (k + 1023) // 1024
        scores(2 * k, sb_ref)
        process(n_full * (1 - later) + (2 * k - 1) * later, sa_ref)
        scores(2 * k + 1, sa_ref)
        process(2 * k, sb_ref)

    later = (n_full // 2 + 1023) // 1024
    held = n_full * (1 - later) + (2 * (n_full // 2) - 1) * later

    @pl.when(n_full % 2 == 1)
    def _():
        scores(n_full - 1, sb_ref)
        process(held, sa_ref)
        process(n_full - 1, sb_ref)

    @pl.when(n_full % 2 == 0)
    def _():
        process(held, sa_ref)

    return acc_ref[...] / jnp.sum(l_ref[...], axis=0, keepdims=True)


CHUNK = 1024
UNITS = 8


class Reduce(Chips):
    def __init__(self, n_tp, txp, rxp, land, peer_sem, ring_sem):
        super().__init__(n_tp)
        self.txp, self.rxp, self.land, self.peer_sem, self.ring_sem = txp, rxp, land, peer_sem, ring_sem
        self.n_chunks = rxp.shape[1]

    def to_other(self, o, j):
        return remote(self.txp.at[o % 2, j], self.rxp.at[o, j], self.peer_sem.at[0, o, j], self.peer_sem.at[1, o, j], tp=self.other)

    def onward(self, o, j):
        odd = o % 2
        return remote(self.rxp.at[o, j], self.land.at[o, j], self.ring_sem.at[0, o, j], self.ring_sem.at[1, o, j],
                      tp=self.right * (1 - odd) + self.left * odd)

    def give(self, o, j, value):
        self.txp[o % 2, j] = value.astype(jnp.bfloat16)
        self.to_other(o, j).start()

    def given(self, o):
        @pl.loop(0, self.n_chunks)
        def _(j):
            self.to_other(o, j).wait_send()

    def keep(self, o, j, value):
        self.to_other(o, j).wait_recv()
        self.rxp[o, j] = (value + self.rxp[o, j].astype(jnp.float32)).astype(jnp.bfloat16)

    def late(self, o, j):
        self.onward(o - 4, j).wait_recv()
        self.rxp[o, j] = (self.rxp[o, j].astype(jnp.float32) + self.land[o - 4, j].astype(jnp.float32)).astype(jnp.bfloat16)

    def total(self, half, j, rows):
        a, b = (4, 3) if half == 0 else (2, 5)
        return (self.rxp[6 + half, j, rows, :].astype(jnp.float32) + self.land[a, j, rows, :].astype(jnp.float32)
                + self.land[b, j, rows, :].astype(jnp.float32)).astype(jnp.bfloat16).astype(jnp.float32)

    def arrive(self, j):
        for o in range(2, 6):
            self.onward(o, j).wait_recv()

    def finish(self):
        @pl.loop(0, self.n_chunks)
        def _(j):
            for o in range(6):
                self.onward(o, j).wait_send()


def rs_scratch(width):
    bf = jnp.bfloat16
    n = width // CHUNK
    return [
        pltpu.VMEM((2, n, 128, CHUNK), bf),
        pltpu.VMEM((UNITS, n, 128, CHUNK), bf),
        pltpu.VMEM((6, n, 128, CHUNK), bf),
        pltpu.SemaphoreType.DMA((2, UNITS, n)),
        pltpu.SemaphoreType.DMA((2, 6, n)),
    ]


def greet_tp(r):
    greet(pltpu.get_barrier_semaphore(), [{'tp': r.other}, {'tp': r.right}, {'tp': r.left}])


def attn_out_kernel(n_tp, n_cp, q_hbm, kv_hbm, wo_hbm, x_ref, g_ref, y_ref, b_ref,
                    q_ref, kv_ref, wo, a_tile, q_tile, sa, sb, p, acc, m, l, sq, w_sem, q_sem, *rs):
    cp = lax.axis_index('cp')
    width = x_ref.shape[1]
    hd = q_tile.shape[0]
    n_heads = q_ref.shape[2]
    piece = n_tp * 128
    n_chunks = width // CHUNK
    red = Reduce(n_tp, *rs)
    loads = [pltpu.make_async_copy(kv_hbm, kv_ref, q_sem.at[0]), pltpu.make_async_copy(q_hbm, q_ref, q_sem.at[1]),
             pltpu.make_async_copy(wo_hbm, wo, w_sem)]
    for c in loads:
        c.start()
    greet_tp(red)
    for c in loads:
        c.wait()

    def order(i):
        first = 1 - i // 4
        turn = 2 * (1 - red.chip // (red.n_chips // 2))
        return first * ((i + turn) % 4) + (1 - first) * i

    @pl.loop(0, 2 * UNITS)
    def _(u):
        o = order(u // 2)
        flip = 1 - u % 2
        slot, half = red.place(o, flip)
        late = slot // (n_tp // 2)
        first = (cp * (1 - late) + (2 * n_cp - 1 - cp) * late) * piece + (slot % (n_tp // 2)) * 256 + half * 128
        for h in range(n_heads):
            q_tile[:, h * 128:(h + 1) * 128] = q_ref[slot, half, h]
        with jax.named_scope('attend'):
            out = attend(q_tile[...], kv_ref, first // KEY_BLOCK, first % KEY_BLOCK, n_cp, n_tp, sa, sb, p, acc, m, l)
        for h in range(n_heads):
            a_tile[:, h * hd:(h + 1) * hd] = out[:, h * 128:(h + 1) * 128].T.astype(jnp.bfloat16)

        def product(j):
            return jnp.dot(a_tile[...], wo[:, chunk(j, CHUNK)], preferred_element_type=jnp.float32)

        @pl.when(flip == 1)
        def _():
            @pl.when(u >= 4)
            def _():
                red.given(order(u // 2 - 2))

            with jax.named_scope('give'):
                @pl.loop(0, n_chunks)
                def _(j):
                    red.give(o, j, product(j))

        @pl.when(flip == 0)
        def _():
            with jax.named_scope('keep'):
                @pl.loop(0, n_chunks)
                def _(j):
                    red.keep(o, j, product(j))

                    @pl.when(o // 2 == 2)
                    def _():
                        red.late(o, j)

                    @pl.when(o < 6)
                    def _():
                        red.onward(o, j).start()

    sq[...] = jnp.zeros_like(sq)

    @pl.loop(0, n_chunks)
    def _(j):
        with jax.named_scope('arrive'):
            red.arrive(j)
        for half in range(2):
            @pl.loop(0, 8)
            def _(r):
                rows = chunk(r, 16)
                at = chunk(half * 8 + r, 16)
                y = (x_ref[at, chunk(j, CHUNK)].astype(jnp.float32) + red.total(half, j, rows)).astype(jnp.bfloat16)
                y_ref[at, chunk(j, CHUNK)] = y
                yf = y.astype(jnp.float32)
                y2 = yf * yf
                sq[at, :] += sum(y2[:, i * 128:(i + 1) * 128] for i in range(CHUNK // 128))

    @pl.loop(0, 16)
    def _(r):
        at = chunk(r, 16)
        scale = lax.rsqrt(jnp.sum(sq[at, :], axis=-1, keepdims=True) / width + NORM_EPS)
        b_ref[at, :] = (y_ref[at, :].astype(jnp.float32) * scale * g_ref[1:2, :]).astype(jnp.bfloat16)
    red.given(6)
    red.given(7)
    red.finish()


def attn_out(q, kv, w_o, x_rows, gains, n_tp, n_cp):
    bf = jnp.bfloat16
    rows, width = x_rows.shape
    n_heads, hd = q.shape[2], q.shape[3]
    nq = n_heads * 128
    return pl.pallas_call(
        functools.partial(attn_out_kernel, n_tp, n_cp),
        out_shape=(jax.ShapeDtypeStruct((rows, width), bf),) * 2,
        in_specs=[HBM, HBM, HBM, VM, VM],
        out_specs=(VM, VM),
        scratch_shapes=[
            pltpu.VMEM(q.shape, bf),
            pltpu.VMEM(kv.shape, bf),
            pltpu.VMEM((n_heads * hd, width), bf),
            pltpu.VMEM((128, n_heads * hd), bf),
            pltpu.VMEM((hd, nq), bf),
            pltpu.VMEM((KEY_BLOCK, nq), jnp.float32),
            pltpu.VMEM((KEY_BLOCK, nq), jnp.float32),
            pltpu.VMEM((KEY_BLOCK, nq), bf),
            pltpu.VMEM((hd, nq), jnp.float32),
            pltpu.VMEM((1, nq), jnp.float32),
            pltpu.VMEM((8, nq), jnp.float32),
            pltpu.VMEM((rows, 128), jnp.float32),
            pltpu.SemaphoreType.DMA(()),
            pltpu.SemaphoreType.DMA((2,)),
            *rs_scratch(width),
        ],
        compiler_params=params(1),
        name='attn_out',
    )(q, kv, w_o, x_rows, gains)


TILE = 256
COLS = 512
N_W = 2
N_D = 3


def mlp_kernel(n_tp, b_hbm, wg_hbm, wu_hbm, wd_hbm, y_hbm, z_hbm, gath, hid, w, wd, ag_send, ag_recv, w_sem, wd_sem, io_sem, z_sem, *rs):
    red = Reduce(n_tp, *rs)
    ag = Gather(n_tp, lambda half: b_hbm.at[pl.ds(half * 128, 128)], gath, ag_send, ag_recv)
    rows, width = b_hbm.shape
    n_tiles = hid.shape[2] // TILE
    n_cols = width // COLS
    per_chunk = CHUNK // COLS
    own_loads = [pltpu.make_async_copy(ag.src(half), ag.part(0, half), io_sem.at[half]) for half in range(2)]
    for c in own_loads:
        c.start()

    def w_load(g, part):
        src = (wg_hbm, wu_hbm)[part]
        return pltpu.make_async_copy(src.at[:, chunk(g % n_tiles, TILE)], w.at[g % N_W, :, pl.ds(part * TILE, TILE)], w_sem.at[g % N_W, part])

    def w_start(g):
        w_load(g, 0).start()
        w_load(g, 1).start()

    def wd_load(c):
        return pltpu.make_async_copy(wd_hbm.at[:, chunk(c % n_cols, COLS)], wd.at[c % N_D], wd_sem.at[c % N_D])

    with jax.named_scope('mgreet'):
        greet_tp(red)
    ag.start(0)
    ag.start(1)
    for g in range(N_W):
        w_start(g)
    for c in range(N_D):
        wd_load(c).start()

    def gate_up(b):
        where = b - 2 * (b // 3)
        base = b * n_tiles

        @pl.loop(0, n_tiles)
        def _(i):
            w_load(base + i, 0).wait()
            w_load(base + i, 1).wait()
            both = jnp.dot(gath[b], w[(base + i) % N_W], preferred_element_type=jnp.float32)
            gate, up = both[:, :TILE], both[:, TILE:]
            hid[where, :, chunk(i, TILE)] = (gate / (1.0 + jnp.exp(-gate)) * up).astype(jnp.bfloat16)
            w_start(base + i + N_W)

    def down(t, pair, flip):
        with jax.named_scope(f'down{t}'):
            down_pass(t, pair, flip)

    def down_pass(t, pair, flip):
        where = (1, 1, 2, 0)[pair]

        @pl.loop(0, n_cols)
        def _(c):
            n = t * n_cols + c
            wd_load(n).wait()
            part = jnp.dot(hid[where, pl.ds(flip * rows, rows), :], wd[n % N_D], preferred_element_type=jnp.float32)
            wd_load(n + N_D).start()
            j, at = c // per_chunk, chunk(c % per_chunk, COLS)
            last = c % per_chunk == per_chunk - 1
            for i in range(2):
                o = 2 * pair + i
                mine = part[i * 128:(i + 1) * 128, :]
                if flip:
                    red.txp[i, j, :, at] = mine.astype(jnp.bfloat16)

                    @pl.when(last)
                    def _():
                        red.to_other(o, j).start()
                else:
                    @pl.when(c % per_chunk == 0)
                    def _():
                        red.to_other(o, j).wait_recv()
                    red.rxp[o, j, :, at] = (mine + red.rxp[o, j, :, at].astype(jnp.float32)).astype(jnp.bfloat16)
                    if pair < 2:
                        @pl.when(last)
                        def _():
                            red.onward(o, j).start()

    def given(pair):
        red.given(2 * pair)
        red.given(2 * pair + 1)

    with jax.named_scope('own'):
        for c in own_loads:
            c.wait()

    @pl.loop(0, 4)
    def _(b):
        for k in range(4):
            @pl.when(b == k)
            def _():
                with jax.named_scope(f'take{k}'):
                    if k == 3:
                        ag.take(k, 0)
                    ag.take(k, 1)
        with jax.named_scope('gate_up'):
            gate_up(b)

        @pl.when(b == 0)
        def _():
            ag.take(1, 0)
            down(0, 3, 1)
            given(3)

        @pl.when(b == 1)
        def _():
            down(1, 1, 1)
            ag.take(2, 0)
            down(2, 1, 0)
            given(1)

    ag.finish()
    y_loads = [pltpu.make_async_copy(y_hbm.at[pl.ds(half * 128, 128)], ag.part(0, half), io_sem.at[half]) for half in range(2)]
    for c in y_loads:
        c.start()
    down(3, 0, 1)
    down(4, 0, 0)
    given(0)
    down(5, 2, 1)
    down(6, 2, 0)
    given(2)
    down(7, 3, 0)
    for i in range(N_D):
        wd_load(UNITS * n_cols + i).wait()
    for i in range(N_W):
        for part in range(2):
            w_load(4 * n_tiles + i, part).wait()

    @pl.loop(0, red.n_chunks)
    def _(j):
        for o in (4, 5):
            red.late(o, j)
            red.onward(o, j).start()
    for c in y_loads:
        c.wait()

    def z_out(j, half):
        return pltpu.make_async_copy(gath.at[0, pl.ds((2 + half) * 128, 128), chunk(j, CHUNK)], z_hbm.at[pl.ds(half * 128, 128), chunk(j, CHUNK)], z_sem.at[half, j])

    @pl.loop(0, red.n_chunks)
    def _(j):
        red.arrive(j)
        for half in range(2):
            @pl.loop(0, 8)
            def _(r):
                at = chunk(r, 16)
                y = gath[0, chunk(half * 8 + r, 16), chunk(j, CHUNK)].astype(jnp.float32)
                gath[0, chunk(16 + half * 8 + r, 16), chunk(j, CHUNK)] = (y + red.total(half, j, at)).astype(jnp.bfloat16)
            z_out(j, half).start()

    @pl.loop(0, red.n_chunks)
    def _(j):
        for half in range(2):
            z_out(j, half).wait()
    red.finish()


def mlp(b, w_gate, w_up, w_down, y_rows, n_tp):
    bf = jnp.bfloat16
    rows, width = b.shape
    ffn = w_gate.shape[1]
    return pl.pallas_call(
        functools.partial(mlp_kernel, n_tp),
        out_shape=jax.ShapeDtypeStruct((rows, width), bf),
        in_specs=[HBM] * 5,
        out_specs=HBM,
        scratch_shapes=[
            pltpu.VMEM((4, 2 * rows, width), bf),
            pltpu.VMEM((3, 2 * rows, ffn), bf),
            pltpu.VMEM((N_W, width, 2 * TILE), bf),
            pltpu.VMEM((N_D, ffn, COLS), bf),
            *Gather.sems(),
            pltpu.SemaphoreType.DMA((N_W, 2)),
            pltpu.SemaphoreType.DMA((N_D,)),
            pltpu.SemaphoreType.DMA((2,)),
            pltpu.SemaphoreType.DMA((2, width // CHUNK)),
            *rs_scratch(width),
        ],
        compiler_params=params(2),
        name='mlp',
    )(b, w_gate, w_up, w_down, y_rows)


def solution(mesh):
    n_cp, n_tp = mesh.shape['cp'], mesh.shape['tp']
    row_spec = P('dp', ('cp', 'tp'), None)
    head_cols = P(None, 'tp', None)

    def local_layer(x, g_attn, w_q, w_k, w_v, w_o, g_mlp, w_gate, w_up, w_down):
        x_rows = x[0]
        gains = jnp.stack([g_attn, g_mlp]).astype(jnp.float32)
        q, kv = ag_qkv(x_rows, gains, w_q, w_k[:, 0], w_v[:, 0], n_tp, n_cp)
        y, b = attn_out(q, kv, w_o.reshape(-1, x_rows.shape[1]), x_rows, gains, n_tp, n_cp)
        return mlp(b, w_gate, w_up, w_down, y, n_tp)[None]

    return jax.shard_map(local_layer, mesh=mesh,
                         in_specs=(row_spec, P(), head_cols, head_cols, head_cols, P('tp', None, None),
                                   P(), P(None, 'tp'), P(None, 'tp'), P('tp', None)),
                         out_specs=row_spec, check_vma=False)
```

time: 974 us -> 450 us (0.46)
  Pallas kernels: 0 us -> 443 us
  waiting for transfers between devices: 433 us -> 0 us
  matrix products: 366 us -> 0 us
  other arithmetic: 114 us -> 1.76 us
  local copies, waits for them, and re-layouts: 33.5 us -> 4.84 us
  between operations: 13.9 us -> 0.04 us
    pallas_call x0 -> x3, Pallas kernels: none -> 443 us  [the longest x1 203 us: mlp(): pl.pallas_call(functools.partial(mlp_kernel, n_tp), out_shape=jax.ShapeDt...]
    dot_general x22 -> x0, matrix products: 350 us -> none  [the longest x8 85.7 us: one_tile(): jnp.einsum('gqrk,kgd->gqrd', weights.astype(jnp.bfloat16), values, prefer...]
    reduce_scatter x2 -> x0, waiting for transfers between devices: 217 us -> none  [the longest x1 109 us: local_layer(): lax.psum_scatter(down_part, 'tp', scatter_dimension=0, tiled=True)]
    all_gather x4 -> x0, waiting for transfers between devices: 215 us -> none  [the longest x1 104 us: local_layer(): normed = lax.all_gather(rms_norm(x_rows, g_attn), 'tp', axis=0, tiled=True)]
    reduce_sum x10 -> x0, other arithmetic: 84.5 us -> none  [the longest x8 78.4 us: one_tile(): row_sum = jnp.sum(weights, axis=-1, keepdims=True)]
    unnamed x1 -> x0, matrix products: 15.7 us -> none
    convert_element_type x8 -> x2, other arithmetic: 15.6 us -> 0.74 us  [the longest x1 0.66 us: local_layer(): gains = jnp.stack([g_attn, g_mlp]).astype(jnp.float32)]
    unnamed x18 -> x1, local copies, waits for them, and re-layouts: 14.1 us -> 3.4 us
  transfers between devices with their start and end apart: 6 -> 0, of which waited for: 5 -> 0; matrix products, arithmetic and copies ran while one was open for 5% -> 0% of each run, Pallas kernels for 0% -> 0%
where the time goes in v1:
time: 450 us
  Pallas kernels  443 us (98%)
  local copies, waits for them, and re-layouts  4.84 us (1%)
    pallas_call x1, Pallas kernels, mlp(): pl.pallas_call(functools.partial(mlp_kernel, n_tp), out_shape=jax.ShapeDt...  203 us
    pallas_call x1, Pallas kernels, attn_out(): pl.pallas_call(functools.partial(attn_out_kernel, n_tp, n_cp), out_shape=...  127 us
    pallas_call x1, Pallas kernels, ag_qkv(): pl.pallas_call(functools.partial(ag_qkv_kernel, n_tp, n_cp, n_heads), out...  114 us

profile of v1, /device:TPU:97, one launch (start us, length us, event | category | flops | bytes accessed | tf_op | source)
XLA Modules:
  0.0 449.9 jit_solution(18019075038876963621)
XLA Ops:
  0.0 0.1 add_convert_fusion
  0.1 0.7 stack.9
  0.8 0.7 stack.10
  1.5 0.7 maximum_convert_fusion.g_ref
  2.2 1.0 fusion
  3.2 113.5 %ag_qkv.1 = (bf16[8,2,4,128,128]{4,3,2,1,0:T(8,128)(2,1)}, bf16[4,8,2,2,128,128]{5,4,3,2,1,0:T(8,128)(2,1)}) custom-call(bf16[256,5120]{1,0:T(8,128)(2,1)} %bitcast.5, f32[2,5120]{1,0:T(2,128)} %maximum_convert_fusion.g_ref, bf16[5120,4,128]{2,1,0:T(4,128)(2,1)} %wq_hbm.1, bf16[5120,128]{1,0:T(8,128)(2,1)} %bitcast.9, bf16[5120,128]{1,0:T(8,128)(2,1)} %bitcast.10, ...), custom_call_target="tpu_custom_call" | custom-call | tf_op jit(solution)/shard_map/ag_qkv/pallas_call | solution.py:248
  116.8 126.9 %attn_out.1 = (bf16[256,5120]{1,0:T(8,128)(2,1)}, bf16[256,5120]{1,0:T(8,128)(2,1)}) custom-call(bf16[8,2,4,128,128]{4,3,2,1,0:T(8,128)(2,1)} %get-tuple-element.9.q_hbm, bf16[4,8,2,2,128,128]{5,4,3,2,1,0:T(8,128)(2,1)} %get-tuple-element.10.kv_hbm, bf16[512,5120]{1,0:T(8,128)(2,1)} %bitcast.8, bf16[256,5120]{1,0:T(8,128)(2,1)} %bitcast.6, ...), custom_call_target="tpu_custom_call" | custom-call | tf_op jit(solution)/shard_map/attn_out/pallas_call | solution.py:505
  243.7 202.8 %mlp.1 = bf16[256,5120]{1,0:T(8,128)(2,1)} custom-call(bf16[256,5120]{1,0:T(8,128)(2,1)} %get-tuple-element.11.b_hbm, bf16[5120,1792]{1,0:T(8,128)(2,1)} %wg_hbm.1, bf16[5120,1792]{1,0:T(8,128)(2,1)} %wu_hbm.1, bf16[1792,5120]{1,0:T(8,128)(2,1)} %wd_hbm.1, bf16[256,5120]{1,0:T(8,128)(2,1)} %get-tuple-element.12.y_hbm), custom_call_target="tpu_custom_call" | custom-call | tf_op jit(solution)/shard_map/mlp/pallas_call | solution.py:699
  446.5 3.4 copy.12
  (3 shorter events, 0.0 us)

commit v2 on v1

v2 whole, which is shorter than its diff:
```python
import functools

import jax
import jax.numpy as jnp
from jax import lax
from jax.experimental import pallas as pl
from jax.experimental.pallas import tpu as pltpu
from jax.sharding import PartitionSpec as P

NORM_EPS = 1e-5
ROPE_THETA = 500000.0
MESH = pl.DeviceIdType.MESH
VMEM_LIMIT = 67_000_000
LOG2E = 1.4426950408889634
BLOCK = 128
SUB = 16
HIGH = 1024
VM = pl.BlockSpec(memory_space=pltpu.VMEM)
HBM = pl.BlockSpec(memory_space=pl.ANY)


def params(ident):
    return pltpu.CompilerParams(collective_id=ident, has_side_effects=True, vmem_limit_bytes=VMEM_LIMIT)


def remote(src, dst, send_sem, recv_sem, **where):
    return pltpu.make_async_remote_copy(
        src_ref=src, dst_ref=dst, send_sem=send_sem, recv_sem=recv_sem,
        device_id=where, device_id_type=MESH)


def ring(n_tp):
    n_chips = n_tp // 2
    me = lax.axis_index('tp')
    chip, core = me // 2, me % 2
    other = chip * 2 + (1 - core)
    right = ((chip + 1) % n_chips) * 2 + core
    left = ((chip + n_chips - 1) % n_chips) * 2 + core
    return me, chip, core, other, right, left


def greet(barrier, partners, meanwhile=lambda: None):
    for where in partners:
        pl.semaphore_signal(barrier, inc=1, device_id=where, device_id_type=MESH)
    meanwhile()
    pl.semaphore_wait(barrier, len(partners))


def unit_place(o):
    far = (7 - o) // 6
    near = o // 6
    offset = 2 * far + (1 - far - near) * (1 - 2 * (o % 2))
    half = (o % 2 + ((o // 2) % 2) * (1 - o // 4)) % 2
    return offset, half


def pair_of(b):
    mid = ((b + 1) // 2) % 2
    return mid * b + (1 - mid) * (3 - b)


class Chips:
    def __init__(self, n_tp):
        self.n_chips = n_tp // 2
        self.me, self.chip, self.core, self.other, self.right, self.left = ring(n_tp)

    def place(self, o, flip):
        offset, half = unit_place(o)
        return ((self.chip + offset + self.n_chips) % self.n_chips) * 2 + (self.core + flip) % 2, half


class Gather(Chips):
    def __init__(self, n_tp, src, gath, send_sem, recv_sem):
        super().__init__(n_tp)
        self.src, self.gath, self.send_sem, self.recv_sem = src, gath, send_sem, recv_sem

    @staticmethod
    def sems():
        return [pltpu.SemaphoreType.DMA((2, 4, 4)), pltpu.SemaphoreType.DMA((4, 4))]

    def part(self, b, e):
        return self.gath.at[b, pl.ds(e * BLOCK, BLOCK)]

    def copy(self, src, b, e, dst, lane=1):
        return remote(src, self.part(b, e), self.send_sem.at[lane, b, e], self.recv_sem.at[b, e], tp=dst)

    def start(self, half):
        self.copy(self.src(half), 1, 1 - half, (self.right, self.left)[half]).start()
        self.copy(self.src(half), 0, 2 + half, self.other, 0).start()
        if half:
            self.copy(self.src(1), 2, 1, self.right).start()
            self.copy(self.src(0), 2, 0, self.left).start()

    def take(self, b, flip):
        for i in range(2):
            e = 2 * flip + i
            here = self.part(b, e)
            if flip or b:
                self.copy(here, b, e, self.other).wait_recv()
            if b and not flip:
                if b == 1:
                    self.copy(here, 3, 1 - i, (self.left, self.right)[i]).start()
                self.copy(here, b, 2 + i, self.other, 0).start()

    def finish(self):
        for i in range(2):
            for b in range(4):
                self.copy(self.src(0), b, 2 + i, self.other, 0).wait_send()
                if b:
                    self.copy(self.src(0), b, i, self.other).wait_send()


def chunk(j, size):
    return pl.ds(j * size if isinstance(j, int) else pl.multiple_of(j * size, size), size)


KEY_BLOCK = 512
HIDDEN = -1e30
EXP_ROWS = 64


class Attend:
    def __init__(self, q_tile, kv_ref, n_cp, n_tp, buffers, p_ref, acc_ref, m_ref, l_ref):
        self.q_tile, self.kv_ref, self.n_cp, self.n_tp = q_tile, kv_ref, n_cp, n_tp
        self.buffers, self.p_ref, self.acc_ref, self.m_ref, self.l_ref = buffers, p_ref, acc_ref, m_ref, l_ref
        self.c = LOG2E * q_tile.shape[0] ** -0.5

    def reset(self):
        self.acc_ref[...] = jnp.zeros_like(self.acc_ref)
        self.m_ref[...] = jnp.full(self.m_ref.shape, HIDDEN, jnp.float32)
        self.l_ref[...] = jnp.zeros_like(self.l_ref)

    def place(self, n):
        per_piece = self.n_tp * BLOCK // KEY_BLOCK
        piece = n // per_piece
        late = piece // self.n_cp
        block = piece * (1 - late) + (2 * self.n_cp - 1 - piece) * late
        return block, (n % per_piece) * (KEY_BLOCK // 256) + late * (self.n_tp // 2)

    def scores(self, n, dst, shift=None):
        j, t = self.place(n)
        q = self.q_tile[...]
        keys = self.kv_ref[j, pl.ds(t, KEY_BLOCK // 256), :, 0].reshape(KEY_BLOCK, q.shape[0])
        s = jnp.dot(keys, q, preferred_element_type=jnp.float32)
        if shift is not None:
            row = lax.broadcasted_iota(jnp.int32, s.shape, 1) % BLOCK
            s = jnp.where(lax.broadcasted_iota(jnp.int32, s.shape, 0) <= row + shift, s, HIDDEN)
        dst[...] = s

    def process(self, n, s_ref):
        j, t = self.place(n)
        nq = s_ref.shape[1]
        m8 = jnp.max(s_ref[...].reshape(-1, 8, nq), axis=0)
        m = self.m_ref[...]
        m_new = jnp.maximum(m, jnp.max(m8, axis=0, keepdims=True))
        self.m_ref[...] = m_new
        alpha = jnp.exp2((m - m_new) * self.c)
        mc = m_new * self.c
        l8 = self.l_ref[...] * alpha
        for r in range(0, KEY_BLOCK, EXP_ROWS):
            p = jnp.exp2(s_ref[r:r + EXP_ROWS, :] * self.c - mc)
            l8 = l8 + jnp.sum(p.reshape(-1, 8, nq), axis=0)
            self.p_ref[r:r + EXP_ROWS, :] = p.astype(jnp.bfloat16)
        self.l_ref[...] = l8
        v_t = jnp.concatenate([self.kv_ref[j, t + i // 2, i % 2, 1] for i in range(KEY_BLOCK // BLOCK)], axis=1)
        self.acc_ref[...] = self.acc_ref[...] * alpha + jnp.dot(v_t, self.p_ref[...], preferred_element_type=jnp.float32)

    def sweep(self, start, shift, count, base, step):
        sa, sb = self.buffers

        self.scores(start, sa, shift)

        @pl.loop(0, count // 2)
        def _(k):
            fresh = 1 - (k + HIGH - 1) // HIGH
            self.scores(base + step * 2 * k, sb)
            self.process(fresh * start + (1 - fresh) * (base + step * (2 * k - 1)), sa)
            self.scores(base + step * (2 * k + 1), sa)
            self.process(base + step * 2 * k, sb)

        even = count // 2 * 2
        fresh = 1 - (even + HIGH - 1) // HIGH
        held = fresh * start + (1 - fresh) * (base + step * (even - 1))

        @pl.when(count % 2 == 1)
        def _():
            self.scores(base + step * even, sb)
            self.process(held, sa)
            self.process(base + step * even, sb)

        @pl.when(count % 2 == 0)
        def _():
            self.process(held, sa)

    def sweep_if_any(self, count, base, step):
        @pl.when(count > 0)
        def _():
            self.sweep(base, None, count - 1, base + step, step)

    def result(self):
        return self.acc_ref[...] / jnp.sum(self.l_ref[...], axis=0, keepdims=True)


CHUNK = 1024
UNITS = 8


class Reduce(Chips):
    def __init__(self, n_tp, n_chunks, txp, rxp, land, peer_sem, ring_sem):
        super().__init__(n_tp)
        self.n_chunks = n_chunks
        self.txp = lambda o, j: txp.at[o % 2, :, chunk(j, CHUNK)]
        self.rxp = lambda o, j: rxp(o).at[:, chunk(j, CHUNK)]
        self.land = lambda o, j: land(o).at[:, chunk(j, CHUNK)]
        self.peer_sem, self.ring_sem = peer_sem, ring_sem

    def to_other(self, o, j):
        return remote(self.txp(o, j), self.rxp(o, j), self.peer_sem.at[0, o, j], self.peer_sem.at[1, o, j], tp=self.other)

    def onward(self, o, j):
        odd = o % 2
        return remote(self.rxp(o, j), self.land(o, j), self.ring_sem.at[0, o, j], self.ring_sem.at[1, o, j],
                      tp=self.right * (1 - odd) + self.left * odd)

    def give(self, o, j, value):
        self.txp(o, j)[...] = value.astype(jnp.bfloat16)
        self.to_other(o, j).start()

    def given(self, o):
        @pl.loop(0, self.n_chunks)
        def _(j):
            self.to_other(o, j).wait_send()

    def keep(self, o, j, value):
        self.to_other(o, j).wait_recv()
        self.rxp(o, j)[...] = (value + self.rxp(o, j)[...].astype(jnp.float32)).astype(jnp.bfloat16)

    def late(self, o, j):
        self.onward(o - 4, j).wait_recv()
        self.rxp(o, j)[...] = (self.rxp(o, j)[...].astype(jnp.float32) + self.land(o - 4, j)[...].astype(jnp.float32)).astype(jnp.bfloat16)

    def total(self, half, j, rows):
        parts = self.rxp(6 + half, j), self.land((4, 2)[half], j), self.land((3, 5)[half], j)
        return sum(p[rows, :].astype(jnp.float32) for p in parts).astype(jnp.bfloat16).astype(jnp.float32)

    def arrive(self, j):
        for o in range(2, 6):
            self.onward(o, j).wait_recv()

    def finish(self):
        @pl.loop(0, self.n_chunks)
        def _(j):
            for o in range(6):
                self.onward(o, j).wait_send()


def rs_sems(n_chunks):
    return [pltpu.SemaphoreType.DMA((2, UNITS, n_chunks)), pltpu.SemaphoreType.DMA((2, 6, n_chunks))]


def greet_tp(r):
    greet(pltpu.get_barrier_semaphore(), [{'tp': r.other}, {'tp': r.right}, {'tp': r.left}])


def scaled(ref, scale, gain_ref, lane):
    return ref.astype(jnp.float32) * scale * gain_ref[lane:lane + 1, :].astype(jnp.float32)


def attn_kernel(n_tp, n_cp, n_heads, x_ref, ga_ref, gm_ref, wq_hbm, wk_hbm, wv_hbm, wo_hbm, cos_ref, sin_ref, y_hbm, b_hbm,
                gath, wraw, wcat, q_ref, kv_ref, wo, y_ref, b_ref, a_tile, q_tile, sa, sb, p, acc, m, l, sq, txp,
                ag_send, ag_recv, kv_send, kv_recv, local, out_sem, free, *rs):
    ag = Gather(n_tp, lambda half: gath.at[0, pl.ds(half * BLOCK, BLOCK)], gath, ag_send, ag_recv)
    width = gath.shape[2]
    n_chunks = width // CHUNK
    unit = lambda o: gath.at[o // 4, chunk(o % 4, BLOCK)]
    red = Reduce(n_tp, n_chunks, txp, unit, lambda o: unit(o + UNITS), *rs)
    cp = lax.axis_index('cp')
    up, down = (cp + 1) % n_cp, (cp + n_cp - 1) % n_cp
    hd = BLOCK
    qw = n_heads * hd
    n_pieces = q_ref.shape[0]
    n_steps = n_pieces // 2
    lanes = range(width // BLOCK)
    tp_partners = [{'tp': ag.other}, {'tp': ag.right}, {'tp': ag.left}]

    loads = [
        pltpu.make_async_copy(wq_hbm, wraw, local.at[0]),
        pltpu.make_async_copy(wk_hbm, wcat.at[:, pl.ds(qw, hd)], local.at[1]),
        pltpu.make_async_copy(wv_hbm, wcat.at[:, pl.ds(qw + hd, hd)], local.at[2]),
        pltpu.make_async_copy(wo_hbm, wo, local.at[3]),
    ]
    for c in loads:
        c.start()

    def norm(half):
        @pl.loop(0, 8)
        def _(r):
            x = x_ref[chunk(half * 8 + r, SUB), :].astype(jnp.float32)
            scale = lax.rsqrt(jnp.sum(x * x, axis=-1, keepdims=True) / width + NORM_EPS)
            for i in lanes:
                at = slice(i * BLOCK, (i + 1) * BLOCK)
                gath[0, chunk(half * 8 + r, SUB), at] = scaled(x[:, at], scale, ga_ref, i).astype(jnp.bfloat16)

    greet(pltpu.get_barrier_semaphore(), [*tp_partners, {'cp': up}, {'cp': down}], lambda: norm(0))
    ag.start(0)
    norm(1)
    ag.start(1)

    def place(n):
        return ag.place(2 * pair_of(n // 4) + n % 2, (n // 2) % 2)

    def kv_copy(where, n, kind, lane, dst):
        slot, half = place(n)
        piece = kv_ref.at[where, slot, half]
        return remote(piece, piece, kv_send.at[lane, n], kv_recv.at[kind, n], cp=dst)

    def kv_forward(n):
        kv_copy(down, n, 0, 0, up).wait_recv()
        kv_copy(up, n, 1, 0, up).wait_recv()
        odd = n % 2
        kv_copy(down * (1 - odd) + up * odd, n, 2, 2, up * (1 - odd) + down * odd).start()

    for c in loads:
        c.wait()

    with jax.named_scope('wcat'):
        @pl.loop(0, wraw.shape[0] // BLOCK)
        def _(i):
            block = wraw[chunk(i, BLOCK)]
            for h in range(n_heads):
                wcat[chunk(i, BLOCK), h * hd:(h + 1) * hd] = block[:, h, :]

    def kv_far(begin, end):
        @pl.loop(begin, end)
        def _(n):
            kv_copy((cp + 2) % n_cp, n, 2, 0, up).wait_recv()

    def order(i):
        o = (1 - i // 4) * ((i + 2) % 4) + i // 4 * i
        swap = 1 - (red.chip + 1) // 2 % 2
        return o + swap * (1 - 2 * (o % 2))

    def tile(o, flip):
        slot, half = red.place(o, flip)
        late = slot // (n_tp // 2)
        first = ((cp * (1 - late) + (2 * n_cp - 1 - cp) * late) * n_tp + slot % (n_tp // 2) * 2 + half) * BLOCK
        for h in range(n_heads):
            q_tile[:, h * BLOCK:(h + 1) * BLOCK] = q_ref[4 * pair_of(o // 2) + 2 * flip + o % 2, h]
        work = Attend(q_tile, kv_ref, n_cp, n_tp, (sa, sb), p, acc.at[flip], m.at[flip], l.at[flip])
        return work, first // KEY_BLOCK, first % KEY_BLOCK

    def far_blocks(n_full):
        half = red.n_chips // 2
        per_half = n_cp * half
        far_late = 1 - red.chip // half
        early = n_full - (n_full // per_half) * (n_full - per_half)
        late = n_full - early
        mixed = far_late * late + (1 - far_late) * early
        at, parity = far_late * per_half, red.chip % half
        return (((mixed - parity + 1) // 2, at + parity, 2),
                ((n_full - mixed, per_half - at, 1), ((mixed + parity) // 2, at + 1 - parity, 2)))

    fine = pl.ds(cos_ref.shape[0] - BLOCK, BLOCK)

    @pl.loop(0, n_steps)
    def _(s):
        for k in range(n_steps):
            @pl.when(s == k)
            def _():
                with jax.named_scope(f'take{k}'):
                    ag.take(k // 2, k % 2)
        product = jnp.dot(gath[s // 2, chunk(s % 2, 256), :], wcat[...], preferred_element_type=jnp.float32)
        for i in range(2):
            n = 2 * s + i
            slot, half = place(n)
            part = product[i * BLOCK:(i + 1) * BLOCK, :]
            coarse = pl.ds(slot * 2 + half, 1)
            cos0, sin0 = cos_ref[coarse, :], sin_ref[coarse, :]
            cos = cos0 * cos_ref[fine, :] - sin0 * sin_ref[fine, :]
            sin = sin0 * cos_ref[fine, :] + cos0 * sin_ref[fine, :]

            def rope(t):
                t = t.astype(jnp.bfloat16).astype(jnp.float32)
                return (t * cos + pltpu.roll(t, hd // 2, 1) * sin).astype(jnp.bfloat16)

            kv_ref[cp, slot, half, 0] = rope(part[:, qw:qw + hd])
            kv_ref[cp, slot, half, 1] = part[:, qw + hd:].T.astype(jnp.bfloat16)
            for h in range(n_heads):
                q_ref[n, h] = rope(part[:, h * hd:(h + 1) * hd]).astype(jnp.float32).T.astype(jnp.bfloat16)
        for i in range(2):
            kv_copy(cp, 2 * s + i, 0, 0, up).start()
            kv_copy(cp, 2 * s + i, 1, 1, down).start()

        @pl.when((s >= 1) & (s != n_steps - 2))
        def _():
            kv_forward(2 * s - 2)
            kv_forward(2 * s - 1)

        @pl.when(s == n_steps - 3)
        def _():
            with jax.named_scope('early'):
                kv_forward(2 * s)
                kv_forward(2 * s + 1)
                kv_far(0, n_pieces - 4)
                o = order(0)
                for flip in (1, 0):
                    work, n_full, _ = tile(o, flip)
                    far, others = far_blocks(n_full)
                    work.reset()
                    for blocks in others:
                        work.sweep_if_any(*blocks)

    ag.finish()
    for where in tp_partners:
        pl.semaphore_signal(free, inc=1, device_id=where, device_id_type=MESH)
    with jax.named_scope('kvtail'):
        for n in range(n_pieces - 2, n_pieces):
            kv_forward(n)

        kv_far(n_pieces - 4, n_pieces)
    pl.semaphore_wait(free, len(tp_partners))

    @pl.loop(0, 2 * UNITS)
    def _(u):
        o = order(u // 2)
        flip = 1 - u % 2
        work, n_full, shift = tile(o, flip)
        begun = 1 - (u + 2 * UNITS - 2) // (2 * UNITS)
        far, _ = far_blocks(n_full)

        @pl.when(begun == 0)
        def _():
            work.reset()
        with jax.named_scope('attend'):
            work.sweep(n_full, shift, *(begun * f + (1 - begun) * w for f, w in zip(far, (n_full, 0, 1))))
        out = work.result()
        for h in range(n_heads):
            a_tile[:, h * hd:(h + 1) * hd] = out[:, h * BLOCK:(h + 1) * BLOCK].T.astype(jnp.bfloat16)

        def product(j):
            return jnp.dot(a_tile[...], wo[:, chunk(j, CHUNK)], preferred_element_type=jnp.float32)

        @pl.when(flip == 1)
        def _():
            @pl.when(u >= 4)
            def _():
                red.given(order(u // 2 - 2))

            with jax.named_scope('give'):
                @pl.loop(0, n_chunks)
                def _(j):
                    red.give(o, j, product(j))

        @pl.when(flip == 0)
        def _():
            with jax.named_scope('keep'):
                @pl.loop(0, n_chunks)
                def _(j):
                    red.keep(o, j, product(j))

                    @pl.when(o < 4)
                    def _():
                        red.onward(o, j).start()

            @pl.when(u // 2 == 5 + red.chip // (red.n_chips // 2))
            def _():
                with jax.named_scope('late'):
                    @pl.loop(0, n_chunks)
                    def _(j):
                        for o in (4, 5):
                            red.late(o, j)
                            red.onward(o, j).start()

    sq[...] = jnp.zeros_like(sq)

    def y_out(j):
        return pltpu.make_async_copy(y_ref.at[:, chunk(j, CHUNK)], y_hbm.at[:, chunk(j, CHUNK)], out_sem.at[j])

    def b_out(i):
        return pltpu.make_async_copy(b_ref.at[chunk(i, 64)], b_hbm.at[chunk(i, 64)], out_sem.at[n_chunks + i])

    @pl.loop(0, n_chunks)
    def _(j):
        with jax.named_scope('arrive'):
            red.arrive(j)
        for half in range(2):
            @pl.loop(0, 8)
            def _(r):
                at = chunk(half * 8 + r, SUB)
                y = (x_ref[at, chunk(j, CHUNK)].astype(jnp.float32) + red.total(half, j, chunk(r, SUB))).astype(jnp.bfloat16)
                y_ref[at, chunk(j, CHUNK)] = y
                yf = y.astype(jnp.float32)
                y2 = yf * yf
                sq[at, :] += sum(y2[:, i * BLOCK:(i + 1) * BLOCK] for i in range(CHUNK // BLOCK))
        y_out(j).start()

    @pl.loop(0, SUB)
    def _(r):
        at = chunk(r, SUB)
        scale = lax.rsqrt(jnp.sum(sq[at, :], axis=-1, keepdims=True) / width + NORM_EPS)
        for i in lanes:
            to = slice(i * BLOCK, (i + 1) * BLOCK)
            b_ref[at, to] = scaled(y_ref[at, to], scale, gm_ref, i).astype(jnp.bfloat16)

        @pl.when(r % 4 == 3)
        def _():
            b_out(r // 4).start()

    @pl.loop(0, n_chunks)
    def _(j):
        y_out(j).wait()
    for i in range(4):
        b_out(i).wait()

    @pl.loop(0, n_pieces)
    def _(n):
        for lane in range(3):
            kv_copy(cp, n, 0, lane, up).wait_send()
    red.given(6)
    red.given(7)
    red.finish()


def attn(x_rows, g_attn, g_mlp, w_q, w_k, w_v, w_o, n_tp, n_cp):
    rows, width = x_rows.shape
    n_heads, hd = w_q.shape[1:]
    bf = jnp.bfloat16
    nq = n_heads * BLOCK
    n = jnp.arange(2 * n_tp, dtype=jnp.int32)
    late = n // n_tp
    cp = lax.axis_index('cp')
    firsts = ((cp * (1 - late) + (2 * n_cp - 1 - cp) * late) * n_tp + n % n_tp) * BLOCK
    points = jnp.concatenate([firsts, jnp.arange(BLOCK, dtype=jnp.int32)]).astype(jnp.float32)
    lane = jnp.arange(hd, dtype=jnp.int32)
    freq = ROPE_THETA ** (-2.0 * (lane % (hd // 2)).astype(jnp.float32) / hd)
    angles = points[:, None] * freq[None, :]
    sign = jnp.where(lane < hd // 2, -1.0, 1.0)
    return pl.pallas_call(
        functools.partial(attn_kernel, n_tp, n_cp, n_heads),
        out_shape=(jax.ShapeDtypeStruct((rows, width), bf),) * 2,
        in_specs=[VM, VM, VM, HBM, HBM, HBM, HBM, VM, VM],
        out_specs=(HBM, HBM),
        scratch_shapes=[
            pltpu.VMEM((4, 2 * rows, width), bf),
            pltpu.VMEM(w_q.shape, bf),
            pltpu.VMEM((width, (n_heads + 2) * hd), bf),
            pltpu.VMEM((2 * n_tp, n_heads, hd, BLOCK), bf),
            pltpu.VMEM((n_cp, n_tp, 2, 2, BLOCK, hd), bf),
            pltpu.VMEM(w_o.shape, bf),
            pltpu.VMEM((rows, width), bf),
            pltpu.VMEM((rows, width), bf),
            pltpu.VMEM((BLOCK, n_heads * hd), bf),
            pltpu.VMEM((hd, nq), bf),
            pltpu.VMEM((KEY_BLOCK, nq), jnp.float32),
            pltpu.VMEM((KEY_BLOCK, nq), jnp.float32),
            pltpu.VMEM((KEY_BLOCK, nq), bf),
            pltpu.VMEM((2, hd, nq), jnp.float32),
            pltpu.VMEM((2, 1, nq), jnp.float32),
            pltpu.VMEM((2, 8, nq), jnp.float32),
            pltpu.VMEM((rows, BLOCK), jnp.float32),
            pltpu.VMEM((2, BLOCK, width), bf),
            *Gather.sems(),
            pltpu.SemaphoreType.DMA((3, 2 * n_tp)),
            pltpu.SemaphoreType.DMA((3, 2 * n_tp)),
            pltpu.SemaphoreType.DMA((4,)),
            pltpu.SemaphoreType.DMA((width // CHUNK + 4,)),
            pltpu.SemaphoreType.REGULAR,
            *rs_sems(width // CHUNK),
        ],
        compiler_params=params(0),
        name='attn',
    )(x_rows, g_attn, g_mlp, w_q, w_k, w_v, w_o, jnp.cos(angles), jnp.sin(angles) * sign)


TILE = 256
COLS = 512
N_W = 2
N_D = 3


def mlp_kernel(n_tp, b_hbm, wg_hbm, wu_hbm, wd_hbm, y_hbm, z_hbm, gath, hid, w, wd, ag_send, ag_recv, w_sem, wd_sem, io_sem, z_sem, txp, rxp, land, *rs):
    red = Reduce(n_tp, b_hbm.shape[1] // CHUNK, txp, lambda o: rxp.at[o], lambda o: land.at[o], *rs)
    ag = Gather(n_tp, lambda half: b_hbm.at[pl.ds(half * BLOCK, BLOCK)], gath, ag_send, ag_recv)
    rows, width = b_hbm.shape
    n_tiles = hid.shape[2] // TILE
    n_cols = width // COLS
    per_chunk = CHUNK // COLS
    own_loads = [pltpu.make_async_copy(ag.src(half), ag.part(0, half), io_sem.at[half]) for half in range(2)]
    for c in own_loads:
        c.start()

    def w_load(g, part):
        src = (wg_hbm, wu_hbm)[part]
        return pltpu.make_async_copy(src.at[:, chunk(g % n_tiles, TILE)], w.at[g % N_W, :, pl.ds(part * TILE, TILE)], w_sem.at[g % N_W, part])

    def w_start(g):
        w_load(g, 0).start()
        w_load(g, 1).start()

    def wd_load(c):
        return pltpu.make_async_copy(wd_hbm.at[:, chunk(c % n_cols, COLS)], wd.at[c % N_D], wd_sem.at[c % N_D])

    with jax.named_scope('mgreet'):
        greet_tp(red)
    ag.start(0)
    ag.start(1)
    for g in range(N_W):
        w_start(g)
    for c in range(N_D):
        wd_load(c).start()

    def gate_up(b):
        where = b - 2 * (b // 3)
        base = b * n_tiles

        @pl.loop(0, n_tiles)
        def _(i):
            w_load(base + i, 0).wait()
            w_load(base + i, 1).wait()
            both = jnp.dot(gath[b], w[(base + i) % N_W], preferred_element_type=jnp.float32)
            gate, up = both[:, :TILE], both[:, TILE:]
            hid[where, :, chunk(i, TILE)] = (gate / (1.0 + jnp.exp(-gate)) * up).astype(jnp.bfloat16)
            w_start(base + i + N_W)

    def down(t, pair, flip):
        with jax.named_scope(f'down{t}'):
            down_pass(t, pair, flip)

    def down_pass(t, pair, flip):
        where = (1, 1, 2, 0)[pair]

        @pl.loop(0, n_cols)
        def _(c):
            n = t * n_cols + c
            wd_load(n).wait()
            part = jnp.dot(hid[where, pl.ds(flip * rows, rows), :], wd[n % N_D], preferred_element_type=jnp.float32)
            wd_load(n + N_D).start()
            j = c // per_chunk
            last = c % per_chunk == per_chunk - 1
            for i in range(2):
                o = 2 * pair + i
                mine = part[i * BLOCK:(i + 1) * BLOCK, :]
                if flip:
                    txp[i, :, chunk(c, COLS)] = mine.astype(jnp.bfloat16)

                    @pl.when(last)
                    def _():
                        red.to_other(o, j).start()
                else:
                    @pl.when(c % per_chunk == 0)
                    def _():
                        red.to_other(o, j).wait_recv()
                    rxp[o, :, chunk(c, COLS)] = (mine + rxp[o, :, chunk(c, COLS)].astype(jnp.float32)).astype(jnp.bfloat16)
                    if pair < 2:
                        @pl.when(last)
                        def _():
                            red.onward(o, j).start()

    def given(pair):
        red.given(2 * pair)
        red.given(2 * pair + 1)

    with jax.named_scope('own'):
        for c in own_loads:
            c.wait()

    @pl.loop(0, 4)
    def _(b):
        for k in range(4):
            @pl.when(b == k)
            def _():
                with jax.named_scope(f'take{k}'):
                    if k == 3:
                        ag.take(k, 0)
                    ag.take(k, 1)
        with jax.named_scope('gate_up'):
            gate_up(b)

        @pl.when(b == 0)
        def _():
            ag.take(1, 0)
            down(0, 3, 1)
            given(3)

        @pl.when(b == 1)
        def _():
            down(1, 1, 1)
            ag.take(2, 0)
            down(2, 1, 0)
            given(1)

    ag.finish()
    y_loads = [pltpu.make_async_copy(y_hbm.at[pl.ds(half * BLOCK, BLOCK)], ag.part(0, half), io_sem.at[half]) for half in range(2)]
    for c in y_loads:
        c.start()
    down(3, 0, 1)
    down(4, 0, 0)
    given(0)
    down(5, 2, 1)
    down(6, 2, 0)
    given(2)
    down(7, 3, 0)
    for i in range(N_D):
        wd_load(UNITS * n_cols + i).wait()
    for i in range(N_W):
        for part in range(2):
            w_load(4 * n_tiles + i, part).wait()

    @pl.loop(0, red.n_chunks)
    def _(j):
        for o in (4, 5):
            red.late(o, j)
            red.onward(o, j).start()
    for c in y_loads:
        c.wait()

    def z_out(j, half):
        return pltpu.make_async_copy(gath.at[0, pl.ds((2 + half) * BLOCK, BLOCK), chunk(j, CHUNK)], z_hbm.at[pl.ds(half * BLOCK, BLOCK), chunk(j, CHUNK)], z_sem.at[half, j])

    @pl.loop(0, red.n_chunks)
    def _(j):
        red.arrive(j)
        for half in range(2):
            @pl.loop(0, 8)
            def _(r):
                at = chunk(r, SUB)
                y = gath[0, chunk(half * 8 + r, SUB), chunk(j, CHUNK)].astype(jnp.float32)
                gath[0, chunk(SUB + half * 8 + r, SUB), chunk(j, CHUNK)] = (y + red.total(half, j, at)).astype(jnp.bfloat16)
            z_out(j, half).start()

    @pl.loop(0, red.n_chunks)
    def _(j):
        for half in range(2):
            z_out(j, half).wait()
    red.finish()


def mlp(b, w_gate, w_up, w_down, y_rows, n_tp):
    bf = jnp.bfloat16
    rows, width = b.shape
    ffn = w_gate.shape[1]
    return pl.pallas_call(
        functools.partial(mlp_kernel, n_tp),
        out_shape=jax.ShapeDtypeStruct((rows, width), bf),
        in_specs=[HBM] * 5,
        out_specs=HBM,
        scratch_shapes=[
            pltpu.VMEM((4, 2 * rows, width), bf),
            pltpu.VMEM((3, 2 * rows, ffn), bf),
            pltpu.VMEM((N_W, width, 2 * TILE), bf),
            pltpu.VMEM((N_D, ffn, COLS), bf),
            *Gather.sems(),
            pltpu.SemaphoreType.DMA((N_W, 2)),
            pltpu.SemaphoreType.DMA((N_D,)),
            pltpu.SemaphoreType.DMA((2,)),
            pltpu.SemaphoreType.DMA((2, width // CHUNK)),
            pltpu.VMEM((2, BLOCK, width), bf),
            pltpu.VMEM((UNITS, BLOCK, width), bf),
            pltpu.VMEM((6, BLOCK, width), bf),
            *rs_sems(width // CHUNK),
        ],
        compiler_params=params(2),
        name='mlp',
    )(b, w_gate, w_up, w_down, y_rows)


def solution(mesh):
    n_cp, n_tp = mesh.shape['cp'], mesh.shape['tp']
    row_spec = P('dp', ('cp', 'tp'))
    cols = P(None, 'tp')

    def local_layer(x, g_attn, w_q, w_k, w_v, w_o, g_mlp, w_gate, w_up, w_down):
        x_rows = x[0]
        width = x_rows.shape[1]
        y, b = attn(x_rows, g_attn.reshape(-1, BLOCK), g_mlp.reshape(-1, BLOCK), w_q, w_k[:, 0], w_v[:, 0], w_o.reshape(-1, width), n_tp, n_cp)
        return mlp(b, w_gate, w_up, w_down, y, n_tp)[None]

    return jax.shard_map(local_layer, mesh=mesh,
                         in_specs=(row_spec, P(), cols, cols, cols, P('tp'), P(), cols, cols, P('tp')),
                         out_specs=row_spec, check_vma=False)
```

time: 450 us -> 419 us (0.931)
  Pallas kernels: 443 us -> 414 us
    pallas_call x2 -> x1, Pallas kernels: 240 us -> 221 us  [attn(): pl.pallas_call(functools.partial(attn_kernel, n_tp, n_cp, n_heads), out_s...]
    pallas_call x1, Pallas kernels: 203 us -> 194 us  [mlp(): pl.pallas_call(functools.partial(mlp_kernel, n_tp), out_shape=jax.ShapeDt...]
where the time goes in v2:
time: 419 us
  Pallas kernels  414 us (99%)
    pallas_call x1, Pallas kernels, attn(): pl.pallas_call(functools.partial(attn_kernel, n_tp, n_cp, n_heads), out_s...  221 us
    pallas_call x1, Pallas kernels, mlp(): pl.pallas_call(functools.partial(mlp_kernel, n_tp), out_shape=jax.ShapeDt...  194 us

profile of v2, /device:TPU:97, one launch (start us, length us, event | category | flops | bytes accessed | tf_op | source)
XLA Modules:
  0.0 418.9 jit_solution(5251025072445378066)
XLA Ops:
  0.0 0.1 add_convert_fusion
  0.1 1.0 fusion
  1.1 220.8 %attn.1 = (bf16[256,5120]{1,0:T(8,128)(2,1)}, bf16[256,5120]{1,0:T(8,128)(2,1)}) custom-call(bf16[256,5120]{1,0:T(8,128)(2,1)} %bitcast.9, bf16[40,128]{1,0:T(8,128)(2,1)} %bitcast.12, bf16[40,128]{1,0:T(8,128)(2,1)} %bitcast.13, bf16[5120,4,128]{2,1,0:T(4,128)(2,1)} %wq_hbm.1, bf16[5120,128]{1,0:T(8,128)(2,1)} %bitcast.10, bf16[5120,128]{1,0:T(8,128)(2,1)} %bitcast.11, ...), custom_call_target="tpu_custom_call" | custom-call | tf_op jit(solution)/shard_map/attn/pallas_call | solution.py:538
  221.9 193.5 %mlp.1 = bf16[256,5120]{1,0:T(8,128)(2,1)} custom-call(bf16[256,5120]{1,0:T(8,128)(2,1)} %get-tuple-element.7.b_hbm, bf16[5120,1792]{1,0:T(8,128)(2,1)} %wg_hbm.1, bf16[5120,1792]{1,0:T(8,128)(2,1)} %wu_hbm.1, bf16[1792,5120]{1,0:T(8,128)(2,1)} %wd_hbm.1, bf16[256,5120]{1,0:T(8,128)(2,1)} %get-tuple-element.8.y_hbm), custom_call_target="tpu_custom_call" | custom-call | tf_op jit(solution)/shard_map/mlp/pallas_call | solution.py:742
  415.5 3.4 copy.12
  (3 shorter events, 0.0 us)

commit v3 on v2

--- a/solution.py
+++ b/solution.py
@@ -145,21 +145,21 @@
         if shift is not None:
             row = lax.broadcasted_iota(jnp.int32, s.shape, 1) % BLOCK
             s = jnp.where(lax.broadcasted_iota(jnp.int32, s.shape, 0) <= row + shift, s, HIDDEN)
-        dst[...] = s
-
-    def process(self, n, s_ref):
+        dst[0][...] = s
+        dst[1][...] = jnp.max(s.reshape(-1, 8, s.shape[1]), axis=0)
+
+    def process(self, n, src):
         j, t = self.place(n)
-        nq = s_ref.shape[1]
-        m8 = jnp.max(s_ref[...].reshape(-1, 8, nq), axis=0)
+        s_ref, m8 = src
         m = self.m_ref[...]
-        m_new = jnp.maximum(m, jnp.max(m8, axis=0, keepdims=True))
+        m_new = jnp.maximum(m, jnp.max(m8[...], axis=0, keepdims=True))
         self.m_ref[...] = m_new
         alpha = jnp.exp2((m - m_new) * self.c)
         mc = m_new * self.c
         l8 = self.l_ref[...] * alpha
         for r in range(0, KEY_BLOCK, EXP_ROWS):
             p = jnp.exp2(s_ref[r:r + EXP_ROWS, :] * self.c - mc)
-            l8 = l8 + jnp.sum(p.reshape(-1, 8, nq), axis=0)
+            l8 = l8 + jnp.sum(p.reshape(-1, *m8.shape), axis=0)
             self.p_ref[r:r + EXP_ROWS, :] = p.astype(jnp.bfloat16)
         self.l_ref[...] = l8
         v_t = jnp.concatenate([self.kv_ref[j, t + i // 2, i % 2, 1] for i in range(KEY_BLOCK // BLOCK)], axis=1)
@@ -231,13 +231,12 @@
         def _(j):
             self.to_other(o, j).wait_send()
 
-    def keep(self, o, j, value):
-        self.to_other(o, j).wait_recv()
+    def add(self, o, j, value):
         self.rxp(o, j)[...] = (value + self.rxp(o, j)[...].astype(jnp.float32)).astype(jnp.bfloat16)
 
     def late(self, o, j):
         self.onward(o - 4, j).wait_recv()
-        self.rxp(o, j)[...] = (self.rxp(o, j)[...].astype(jnp.float32) + self.land(o - 4, j)[...].astype(jnp.float32)).astype(jnp.bfloat16)
+        self.add(o, j, self.land(o - 4, j)[...].astype(jnp.float32))
 
     def total(self, half, j, rows):
         parts = self.rxp(6 + half, j), self.land((4, 2)[half], j), self.land((3, 5)[half], j)
@@ -247,11 +246,9 @@
         for o in range(2, 6):
             self.onward(o, j).wait_recv()
 
-    def finish(self):
-        @pl.loop(0, self.n_chunks)
-        def _(j):
-            for o in range(6):
-                self.onward(o, j).wait_send()
+    def sent(self, j):
+        for o in range(6):
+            self.onward(o, j).wait_send()
 
 
 def rs_sems(n_chunks):
@@ -266,9 +263,9 @@
     return ref.astype(jnp.float32) * scale * gain_ref[lane:lane + 1, :].astype(jnp.float32)
 
 
-def attn_kernel(n_tp, n_cp, n_heads, x_ref, ga_ref, gm_ref, wq_hbm, wk_hbm, wv_hbm, wo_hbm, cos_ref, sin_ref, y_hbm, b_hbm,
-                gath, wraw, wcat, q_ref, kv_ref, wo, y_ref, b_ref, a_tile, q_tile, sa, sb, p, acc, m, l, sq, txp,
-                ag_send, ag_recv, kv_send, kv_recv, local, out_sem, free, *rs):
+def attn_kernel(n_tp, n_cp, n_heads, x_hbm, ga_ref, gm_ref, wq_hbm, wk_hbm, wv_hbm, wo_hbm, cos_ref, sin_ref, y_hbm, b_hbm,
+                gath, x_ref, wraw, wcat, q_ref, kv_ref, wo, y_ref, b_ref, a_tile, q_tile, sa, sb, m8, p, acc, m, l, sq, txp,
+                ag_send, ag_recv, kv_send, kv_recv, x_sem, local, out_sem, free, *rs):
     ag = Gather(n_tp, lambda half: gath.at[0, pl.ds(half * BLOCK, BLOCK)], gath, ag_send, ag_recv)
     width = gath.shape[2]
     n_chunks = width // CHUNK
@@ -283,16 +280,22 @@
     lanes = range(width // BLOCK)
     tp_partners = [{'tp': ag.other}, {'tp': ag.right}, {'tp': ag.left}]
 
+    def x_load(half):
+        at = pl.ds(half * BLOCK, BLOCK)
+        return pltpu.make_async_copy(x_hbm.at[at], x_ref.at[at], x_sem.at[half])
+
+    x_load(0).start()
+    x_load(1).start()
     loads = [
         pltpu.make_async_copy(wq_hbm, wraw, local.at[0]),
         pltpu.make_async_copy(wk_hbm, wcat.at[:, pl.ds(qw, hd)], local.at[1]),
         pltpu.make_async_copy(wv_hbm, wcat.at[:, pl.ds(qw + hd, hd)], local.at[2]),
         pltpu.make_async_copy(wo_hbm, wo, local.at[3]),
     ]
-    for c in loads:
-        c.start()
 
     def norm(half):
+        x_load(half).wait()
+
         @pl.loop(0, 8)
         def _(r):
             x = x_ref[chunk(half * 8 + r, SUB), :].astype(jnp.float32)
@@ -305,6 +308,8 @@
     ag.start(0)
     norm(1)
     ag.start(1)
+    for c in loads:
+        c.start()
 
     def place(n):
         return ag.place(2 * pair_of(n // 4) + n % 2, (n // 2) % 2)
@@ -346,7 +351,7 @@
         first = ((cp * (1 - late) + (2 * n_cp - 1 - cp) * late) * n_tp + slot % (n_tp // 2) * 2 + half) * BLOCK
         for h in range(n_heads):
             q_tile[:, h * BLOCK:(h + 1) * BLOCK] = q_ref[4 * pair_of(o // 2) + 2 * flip + o % 2, h]
-        work = Attend(q_tile, kv_ref, n_cp, n_tp, (sa, sb), p, acc.at[flip], m.at[flip], l.at[flip])
+        work = Attend(q_tile, kv_ref, n_cp, n_tp, ((sa, m8.at[0]), (sb, m8.at[1])), p, acc.at[flip], m.at[flip], l.at[flip])
         return work, first // KEY_BLOCK, first % KEY_BLOCK
 
     def far_blocks(n_full):
@@ -447,19 +452,20 @@
                 red.given(order(u // 2 - 2))
 
             with jax.named_scope('give'):
-                @pl.loop(0, n_chunks)
-                def _(j):
+                for j in range(n_chunks):
                     red.give(o, j, product(j))
 
         @pl.when(flip == 0)
         def _():
             with jax.named_scope('keep'):
-                @pl.loop(0, n_chunks)
-                def _(j):
-                    red.keep(o, j, product(j))
-
-                    @pl.when(o < 4)
-                    def _():
+                for j in range(n_chunks):
+                    red.to_other(o, j).wait_recv()
+                for j in range(n_chunks):
+                    red.add(o, j, product(j))
+
+                @pl.when(o < 4)
+                def _():
+                    for j in range(n_chunks):
                         red.onward(o, j).start()
 
             @pl.when(u // 2 == 5 + red.chip // (red.n_chips // 2))
@@ -472,6 +478,13 @@
                             red.onward(o, j).start()
 
     sq[...] = jnp.zeros_like(sq)
+
+    @pl.loop(0, n_pieces)
+    def _(n):
+        for lane in range(3):
+            kv_copy(cp, n, 0, lane, up).wait_send()
+    red.given(6)
+    red.given(7)
 
     def y_out(j):
         return pltpu.make_async_copy(y_ref.at[:, chunk(j, CHUNK)], y_hbm.at[:, chunk(j, CHUNK)], out_sem.at[j])
@@ -493,14 +506,16 @@
                 y2 = yf * yf
                 sq[at, :] += sum(y2[:, i * BLOCK:(i + 1) * BLOCK] for i in range(CHUNK // BLOCK))
         y_out(j).start()
+        red.sent(j)
+
+    sq[...] = jnp.broadcast_to(lax.rsqrt(jnp.sum(sq[...], axis=-1, keepdims=True) / width + NORM_EPS), sq.shape)
 
     @pl.loop(0, SUB)
     def _(r):
         at = chunk(r, SUB)
-        scale = lax.rsqrt(jnp.sum(sq[at, :], axis=-1, keepdims=True) / width + NORM_EPS)
         for i in lanes:
             to = slice(i * BLOCK, (i + 1) * BLOCK)
-            b_ref[at, to] = scaled(y_ref[at, to], scale, gm_ref, i).astype(jnp.bfloat16)
+            b_ref[at, to] = scaled(y_ref[at, to], sq[at, :], gm_ref, i).astype(jnp.bfloat16)
 
         @pl.when(r % 4 == 3)
         def _():
@@ -511,14 +526,6 @@
         y_out(j).wait()
     for i in range(4):
         b_out(i).wait()
-
-    @pl.loop(0, n_pieces)
-    def _(n):
-        for lane in range(3):
-            kv_copy(cp, n, 0, lane, up).wait_send()
-    red.given(6)
-    red.given(7)
-    red.finish()
 
 
 def attn(x_rows, g_attn, g_mlp, w_q, w_k, w_v, w_o, n_tp, n_cp):
@@ -538,10 +545,11 @@
     return pl.pallas_call(
         functools.partial(attn_kernel, n_tp, n_cp, n_heads),
         out_shape=(jax.ShapeDtypeStruct((rows, width), bf),) * 2,
-        in_specs=[VM, VM, VM, HBM, HBM, HBM, HBM, VM, VM],
+        in_specs=[HBM, VM, VM, HBM, HBM, HBM, HBM, VM, VM],
         out_specs=(HBM, HBM),
         scratch_shapes=[
             pltpu.VMEM((4, 2 * rows, width), bf),
+            pltpu.VMEM((rows, width), bf),
             pltpu.VMEM(w_q.shape, bf),
             pltpu.VMEM((width, (n_heads + 2) * hd), bf),
             pltpu.VMEM((2 * n_tp, n_heads, hd, BLOCK), bf),
@@ -553,6 +561,7 @@
             pltpu.VMEM((hd, nq), bf),
             pltpu.VMEM((KEY_BLOCK, nq), jnp.float32),
             pltpu.VMEM((KEY_BLOCK, nq), jnp.float32),
+            pltpu.VMEM((2, 8, nq), jnp.float32),
             pltpu.VMEM((KEY_BLOCK, nq), bf),
             pltpu.VMEM((2, hd, nq), jnp.float32),
             pltpu.VMEM((2, 1, nq), jnp.float32),
@@ -562,6 +571,7 @@
             *Gather.sems(),
             pltpu.SemaphoreType.DMA((3, 2 * n_tp)),
             pltpu.SemaphoreType.DMA((3, 2 * n_tp)),
+            pltpu.SemaphoreType.DMA((2,)),
             pltpu.SemaphoreType.DMA((4,)),
             pltpu.SemaphoreType.DMA((width // CHUNK + 4,)),
             pltpu.SemaphoreType.REGULAR,
@@ -572,13 +582,14 @@
     )(x_rows, g_attn, g_mlp, w_q, w_k, w_v, w_o, jnp.cos(angles), jnp.sin(angles) * sign)
 
 
+PLACES = (1, 1, 2, 0)
 TILE = 256
 COLS = 512
 N_W = 2
 N_D = 3
 
 
-def mlp_kernel(n_tp, b_hbm, wg_hbm, wu_hbm, wd_hbm, y_hbm, z_hbm, gath, hid, w, wd, ag_send, ag_recv, w_sem, wd_sem, io_sem, z_sem, txp, rxp, land, *rs):
+def mlp_kernel(n_tp, b_hbm, wg_hbm, wu_hbm, wd_hbm, y_hbm, z_hbm, gath, hid, w, wd, ag_send, ag_recv, w_sem, wd_sem, io_sem, z_sem, mine, txp, rxp, land, *rs):
     red = Reduce(n_tp, b_hbm.shape[1] // CHUNK, txp, lambda o: rxp.at[o], lambda o: land.at[o], *rs)
     ag = Gather(n_tp, lambda half: b_hbm.at[pl.ds(half * BLOCK, BLOCK)], gath, ag_send, ag_recv)
     rows, width = b_hbm.shape
@@ -623,11 +634,7 @@
             w_start(base + i + N_W)
 
     def down(t, pair, flip):
-        with jax.named_scope(f'down{t}'):
-            down_pass(t, pair, flip)
-
-    def down_pass(t, pair, flip):
-        where = (1, 1, 2, 0)[pair]
+        where = PLACES[pair]
 
         @pl.loop(0, n_cols)
         def _(c):
@@ -656,6 +663,38 @@
                         def _():
                             red.onward(o, j).start()
 
+    def down_both(t, pair):
+        where = PLACES[pair]
+
+        def combine(j):
+            for i in range(2):
+                o = 2 * pair + i
+                red.to_other(o, j).wait_recv()
+                red.add(o, j, mine[2 * (j % 2) + i].astype(jnp.float32))
+                if pair < 2:
+                    red.onward(o, j).start()
+
+        @pl.loop(0, n_cols)
+        def _(c):
+            n = t * n_cols + c
+            wd_load(n).wait()
+            part = jnp.dot(hid[where], wd[n % N_D], preferred_element_type=jnp.float32)
+            wd_load(n + N_D).start()
+            j = c // per_chunk
+            for i in range(2):
+                mine[2 * (j % 2) + i, :, chunk(c % per_chunk, COLS)] = part[i * BLOCK:(i + 1) * BLOCK, :].astype(jnp.bfloat16)
+                txp[i, :, chunk(c, COLS)] = part[rows + i * BLOCK:rows + (i + 1) * BLOCK, :].astype(jnp.bfloat16)
+
+            @pl.when(c % per_chunk == per_chunk - 1)
+            def _():
+                for i in range(2):
+                    red.to_other(2 * pair + i, j).start()
+
+                @pl.when(j > 0)
+                def _():
+                    combine(j - 1)
+        combine(red.n_chunks - 1)
+
     def given(pair):
         red.given(2 * pair)
         red.given(2 * pair + 1)
@@ -670,22 +709,24 @@
             @pl.when(b == k)
             def _():
                 with jax.named_scope(f'take{k}'):
-                    if k == 3:
-                        ag.take(k, 0)
                     ag.take(k, 1)
         with jax.named_scope('gate_up'):
             gate_up(b)
 
         @pl.when(b == 0)
         def _():
+            down(0, 3, 1)
             ag.take(1, 0)
-            down(0, 3, 1)
             given(3)
 
         @pl.when(b == 1)
         def _():
+            ag.take(2, 0)
             down(1, 1, 1)
-            ag.take(2, 0)
+
+        @pl.when(b == 2)
+        def _():
+            ag.take(3, 0)
             down(2, 1, 0)
             given(1)
 
@@ -693,15 +734,13 @@
     y_loads = [pltpu.make_async_copy(y_hbm.at[pl.ds(half * BLOCK, BLOCK)], ag.part(0, half), io_sem.at[half]) for half in range(2)]
     for c in y_loads:
         c.start()
-    down(3, 0, 1)
-    down(4, 0, 0)
+    down_both(3, 0)
     given(0)
-    down(5, 2, 1)
-    down(6, 2, 0)
+    down_both(4, 2)
     given(2)
-    down(7, 3, 0)
+    down(5, 3, 0)
     for i in range(N_D):
-        wd_load(UNITS * n_cols + i).wait()
+        wd_load(6 * n_cols + i).wait()
     for i in range(N_W):
         for part in range(2):
             w_load(4 * n_tiles + i, part).wait()
@@ -727,12 +766,12 @@
                 y = gath[0, chunk(half * 8 + r, SUB), chunk(j, CHUNK)].astype(jnp.float32)
                 gath[0, chunk(SUB + half * 8 + r, SUB), chunk(j, CHUNK)] = (y + red.total(half, j, at)).astype(jnp.bfloat16)
             z_out(j, half).start()
+        red.sent(j)
 
     @pl.loop(0, red.n_chunks)
     def _(j):
         for half in range(2):
             z_out(j, half).wait()
-    red.finish()
 
 
 def mlp(b, w_gate, w_up, w_down, y_rows, n_tp):
@@ -754,6 +793,7 @@
             pltpu.SemaphoreType.DMA((N_D,)),
             pltpu.SemaphoreType.DMA((2,)),
             pltpu.SemaphoreType.DMA((2, width // CHUNK)),
+            pltpu.VMEM((4, BLOCK, CHUNK), bf),
             pltpu.VMEM((2, BLOCK, width), bf),
             pltpu.VMEM((UNITS, BLOCK, width), bf),
             pltpu.VMEM((6, BLOCK, width), bf),

time: 419 us -> 408 us (0.974)
  Pallas kernels: 414 us -> 403 us
    pallas_call x1, Pallas kernels: 194 us -> 186 us  [mlp(): pl.pallas_call(functools.partial(mlp_kernel, n_tp), out_shape=jax.ShapeDt...]
where the time goes in v3:
time: 408 us; the launch traced here: 407 us
  Pallas kernels  403 us (99%)
    pallas_call x1, Pallas kernels, attn(): pl.pallas_call(functools.partial(attn_kernel, n_tp, n_cp, n_heads), out_s...  217 us
    pallas_call x1, Pallas kernels, mlp(): pl.pallas_call(functools.partial(mlp_kernel, n_tp), out_shape=jax.ShapeDt...  186 us

profile of v3, /device:TPU:97, one launch (start us, length us, event | category | flops | bytes accessed | tf_op | source)
XLA Modules:
  0.0 407.5 jit_solution(8205362343362502637)
XLA Ops:
  0.0 0.1 add_convert_fusion
  0.1 1.0 fusion
  1.1 217.1 %attn.1 = (bf16[256,5120]{1,0:T(8,128)(2,1)}, bf16[256,5120]{1,0:T(8,128)(2,1)}) custom-call(bf16[256,5120]{1,0:T(8,128)(2,1)} %bitcast.9, bf16[40,128]{1,0:T(8,128)(2,1)} %bitcast.12, bf16[40,128]{1,0:T(8,128)(2,1)} %bitcast.13, bf16[5120,4,128]{2,1,0:T(4,128)(2,1)} %wq_hbm.1, bf16[5120,128]{1,0:T(8,128)(2,1)} %bitcast.10, bf16[5120,128]{1,0:T(8,128)(2,1)} %bitcast.11, ...), custom_call_target="tpu_custom_call" | custom-call | tf_op jit(solution)/shard_map/attn/pallas_call | solution.py:545
  218.2 185.9 %mlp.1 = bf16[256,5120]{1,0:T(8,128)(2,1)} custom-call(bf16[256,5120]{1,0:T(8,128)(2,1)} %get-tuple-element.7.b_hbm, bf16[5120,1792]{1,0:T(8,128)(2,1)} %wg_hbm.1, bf16[5120,1792]{1,0:T(8,128)(2,1)} %wu_hbm.1, bf16[1792,5120]{1,0:T(8,128)(2,1)} %wd_hbm.1, bf16[256,5120]{1,0:T(8,128)(2,1)} %get-tuple-element.8.y_hbm), custom_call_target="tpu_custom_call" | custom-call | tf_op jit(solution)/shard_map/mlp/pallas_call | solution.py:781
  404.1 3.4 copy.12
  (3 shorter events, 0.0 us)
